TPU v7x, 32 devices: a whole 2x2x4 slice. The times are simulated.
32 devices in a mesh: sims: 2 (over x), rows: 4 (over y, core), fields: 4 (over z).
Axes of the slice: x: 2, y: 2, z: 4, core: 2. Of those that a mesh axis runs over, the one named last changes fastest.
Arguments:
- sky_maps: float32 [6, 32, 16384], P('sims', 'rows', 'fields'), parts along dimension 0, may hold values from -7 to 7
- band_cuts: int32 [6], replicated, may hold values from 1 to 8191, as said below
- filters: float32 [3, 32, 16384], P(None, ('rows', 'fields')), may hold values from 0.3 to 3
- wiener: float32 [2, 32, 16384], P(None, ('rows', 'fields')), may hold values from 0.3 to 3
- response: float32 [32, 16384], P(('rows', 'fields')), may hold values from 0.5 to 2
Outputs:
- phi_curl: float32 [4, 32, 16384], P('sims', 'rows', 'fields'), parts along dimension 0
There are 2 independent parts, one for each index of `sims`. A program takes and returns all parts, laid end to end along the dimension named above; an argument that names none is the same for every part. Nothing has to cross between parts.
Inputs may be any that keep to these rules, and one draw needn't show every extreme that they name: `band_cuts`: entries 0, 2 and 4 are the smallest multipole indices of the temperature, polarization and estimate bands and lie below 512; entries 1, 3 and 5 are the largest and are at least 4096.
All inputs are finite; a program needn't handle non-finite values.
Results may differ from a plain program's by a relative error of at most 0.00019.
Values sent between devices are 32-bit elements; how exact they have to be, the bound alone decides.
A program may use at most 128 MiB of HBM per device.

v0:
```python
import math

import jax
import jax.numpy as jnp
from jax import lax
from jax.sharding import PartitionSpec as P

NC = 16384


exact_mode = lax.Precision.HIGHEST


def split_factor(length):
    best_first = 1
    for divisor in range(1, math.isqrt(length) + 1):
        if length % divisor == 0:
            best_first = divisor
    return (best_first, length // best_first)


def phase_table(left_index, right_index, period, direction):
    product = left_index[:, None] * right_index[None, :] % period
    angles = direction * 2.0 * math.pi / period * product.astype(jnp.float32)
    return (jnp.cos(angles), jnp.sin(angles))


def complex_einsum(formula, data_pair, table_pair):
    data_real, data_imag = data_pair
    table_real, table_imag = table_pair
    real_out = jnp.einsum(formula, data_real, table_real, precision=exact_mode)
    imag_out = jnp.einsum(formula, data_real, table_imag, precision=exact_mode)
    if data_imag is not None:
        real_out = real_out - jnp.einsum(formula, data_imag, table_imag, precision=exact_mode)
        imag_out = imag_out + jnp.einsum(formula, data_imag, table_real, precision=exact_mode)
    return (real_out, imag_out)


def complex_mul(left_pair, right_pair):
    return (
        left_pair[0] * right_pair[0] - left_pair[1] * right_pair[1],
        left_pair[0] * right_pair[1] + left_pair[1] * right_pair[0],
    )


def conj_mul(left_pair, right_pair):
    return (
        left_pair[0] * right_pair[0] + left_pair[1] * right_pair[1],
        left_pair[0] * right_pair[1] - left_pair[1] * right_pair[0],
    )


def row_transform(data_pair, direction):
    batch_len, length, block_width = data_pair[0].shape
    outer_len, inner_len = split_factor(length)
    outer_ids = jnp.arange(outer_len, dtype=jnp.int32)
    inner_ids = jnp.arange(inner_len, dtype=jnp.int32)
    real_in = data_pair[0].reshape(batch_len, outer_len, inner_len, block_width)
    imag_in = None
    if data_pair[1] is not None:
        imag_in = data_pair[1].reshape(batch_len, outer_len, inner_len, block_width)
    middle = complex_einsum(
        "bjmc,jk->bkmc", (real_in, imag_in), phase_table(outer_ids, outer_ids, outer_len, direction)
    )
    twiddle = phase_table(outer_ids, inner_ids, length, direction)
    middle = complex_mul(middle, (twiddle[0][None, :, :, None], twiddle[1][None, :, :, None]))
    result = complex_einsum(
        "bkmc,mq->bqkc", middle, phase_table(inner_ids, inner_ids, inner_len, direction)
    )
    norm_factor = 1.0 if direction < 0 else 1.0 / length
    return (
        result[0].reshape(batch_len, length, block_width) * norm_factor,
        result[1].reshape(batch_len, length, block_width) * norm_factor,
    )


def block_order(groups, fields_count):
    positions = jnp.arange(groups, dtype=jnp.int32)
    blocks = positions % fields_count * (groups // fields_count) + positions // fields_count
    return (positions, blocks)


def column_forward(data_pair, groups, fields_count):
    batch_len, local_rows, total_len = data_pair[0].shape
    block_width = total_len // groups
    positions, blocks = block_order(groups, fields_count)
    column_ids = jnp.arange(block_width, dtype=jnp.int32)
    shaped = (
        data_pair[0].reshape(batch_len, local_rows, groups, block_width),
        data_pair[1].reshape(batch_len, local_rows, groups, block_width),
    )
    middle = complex_einsum("brpc,pk->brkc", shaped, phase_table(blocks, positions, groups, -1.0))
    twiddle = phase_table(positions, column_ids, total_len, -1.0)
    middle = complex_mul(middle, (twiddle[0][None, None], twiddle[1][None, None]))
    result = complex_einsum(
        "brkc,cq->brqk", middle, phase_table(column_ids, column_ids, block_width, -1.0)
    )
    return (
        result[0].reshape(batch_len, local_rows, total_len),
        result[1].reshape(batch_len, local_rows, total_len),
    )


def column_inverse(data_pair, groups, fields_count):
    batch_len, local_rows, total_len = data_pair[0].shape
    block_width = total_len // groups
    positions, blocks = block_order(groups, fields_count)
    column_ids = jnp.arange(block_width, dtype=jnp.int32)
    shaped = (
        data_pair[0].reshape(batch_len, local_rows, block_width, groups),
        data_pair[1].reshape(batch_len, local_rows, block_width, groups),
    )
    middle = complex_einsum(
        "brqk,qc->brkc", shaped, phase_table(column_ids, column_ids, block_width, 1.0)
    )
    twiddle = phase_table(positions, column_ids, total_len, 1.0)
    middle = complex_mul(middle, (twiddle[0][None, None], twiddle[1][None, None]))
    result = complex_einsum("brkc,kp->brpc", middle, phase_table(positions, blocks, groups, 1.0))
    norm_factor = 1.0 / total_len
    return (
        result[0].reshape(batch_len, local_rows, total_len) * norm_factor,
        result[1].reshape(batch_len, local_rows, total_len) * norm_factor,
    )


def body(sky_maps, band_cuts, filters, wiener, response):
    rows_count = lax.axis_size("rows")
    fields_count = lax.axis_size("fields")
    groups = rows_count * fields_count
    local_rows = filters.shape[1]
    total_rows = local_rows * groups
    row_ratio = NC // total_rows

    def forward_columns(stacked):
        return jnp.stack(column_forward((stacked[0], stacked[1]), groups, fields_count))

    def inverse_rows(stacked):
        return jnp.stack(row_transform((stacked[0], stacked[1]), 1.0))

    def inverse_columns(stacked):
        return jnp.stack(column_inverse((stacked[0], stacked[1]), groups, fields_count))

    def to_frequency(stacked):
        batch_len = stacked.shape[1]
        block_width = stacked.shape[3]
        shaped = stacked.reshape(
            2, batch_len, rows_count, fields_count, local_rows, 1, 1, block_width
        )
        arrived = lax.all_to_all(
            lax.all_to_all(shaped, "rows", split_axis=2, concat_axis=5, tiled=True),
            "fields",
            split_axis=3,
            concat_axis=6,
            tiled=True,
        )
        result = forward_columns(arrived.reshape(2, batch_len, local_rows, groups * block_width))
        return result

    def to_space(stacked):
        batch_len = stacked.shape[1]
        block_width = stacked.shape[3] // groups
        shaped = stacked.reshape(
            2, batch_len, 1, 1, local_rows, rows_count, fields_count, block_width
        )
        arrived = lax.all_to_all(
            lax.all_to_all(shaped, "rows", split_axis=5, concat_axis=2, tiled=True),
            "fields",
            split_axis=6,
            concat_axis=3,
            tiled=True,
        )
        result = inverse_rows(arrived.reshape(2, batch_len, total_rows, block_width))
        return result

    slab_spectra = jnp.stack(
        row_transform(
            (lax.all_to_all(sky_maps, "rows", split_axis=2, concat_axis=1, tiled=True), None), -1.0
        )
    )
    sky_spectra = to_frequency(slab_spectra)
    row_ids = lax.axis_index(("rows", "fields")) * local_rows + jnp.arange(
        local_rows, dtype=jnp.int32
    )
    freq_rows = jnp.where(row_ids < total_rows // 2, row_ids, row_ids - total_rows)[:, None]
    column_ids = jnp.arange(NC, dtype=jnp.int32)
    freq_cols = jnp.where(column_ids < NC // 2, column_ids, column_ids - NC)[None, :]
    scaled_rows = row_ratio * freq_rows
    radius_sq = freq_cols * freq_cols + scaled_rows * scaled_rows

    def band_mask(lower_cut, upper_cut):
        inside = (radius_sq >= lower_cut * lower_cut) & (radius_sq <= upper_cut * upper_cut)
        return inside.astype(jnp.float32)

    mask_temp = band_mask(band_cuts[0], band_cuts[1])
    mask_pol = band_mask(band_cuts[2], band_cuts[3])
    mask_out = band_mask(band_cuts[4], band_cuts[5])
    radius_floor = jnp.maximum(radius_sq, 1).astype(jnp.float32)
    cos_two = (freq_cols * freq_cols - scaled_rows * scaled_rows).astype(jnp.float32) / radius_floor
    sin_two = (2 * freq_cols * scaled_rows).astype(jnp.float32) / radius_floor
    along_x = (2 * freq_cols).astype(jnp.float32) / NC
    along_y = (2 * freq_rows).astype(jnp.float32) / total_rows
    raising = (-along_y + 0.0 * along_x, along_x + 0.0 * along_y)
    lowering = (along_y + 0.0 * along_x, along_x + 0.0 * along_y)
    rotation = (cos_two, sin_two)
    temp_modes = (sky_spectra[0, 0], sky_spectra[1, 0])
    stokes_q = (sky_spectra[0, 1], sky_spectra[1, 1])
    stokes_u = (sky_spectra[0, 2], sky_spectra[1, 2])
    e_modes = (
        -(cos_two * stokes_q[0] + sin_two * stokes_u[0]),
        -(cos_two * stokes_q[1] + sin_two * stokes_u[1]),
    )
    b_modes = (
        sin_two * stokes_q[0] - cos_two * stokes_u[0],
        sin_two * stokes_q[1] - cos_two * stokes_u[1],
    )
    temp_weight = mask_temp * filters[0]
    e_weight = mask_pol * filters[1]
    b_weight = mask_pol * filters[2]
    temp_bar = (temp_weight * temp_modes[0], temp_weight * temp_modes[1])
    e_bar = (e_weight * e_modes[0], e_weight * e_modes[1])
    b_bar = (b_weight * b_modes[0], b_weight * b_modes[1])
    grad_temp = complex_mul(raising, (wiener[0] * temp_bar[0], wiener[0] * temp_bar[1]))
    pol_sum = complex_mul((e_bar[0] - b_bar[1], e_bar[1] + b_bar[0]), rotation)
    pol_bar = (-pol_sum[0], -pol_sum[1])
    pol_rot = complex_mul((wiener[1] * e_bar[0], wiener[1] * e_bar[1]), rotation)
    pol_wiener = (-pol_rot[0], -pol_rot[1])
    spin_three = complex_mul(raising, pol_wiener)
    spin_one = complex_mul(lowering, pol_wiener)
    leg_spectra = jnp.stack(
        [
            jnp.stack([temp_bar[0], grad_temp[0], pol_bar[0], spin_three[0], spin_one[0]]),
            jnp.stack([temp_bar[1], grad_temp[1], pol_bar[1], spin_three[1], spin_one[1]]),
        ]
    )
    leg_maps = to_space(inverse_columns(leg_spectra))
    temp_leg = (leg_maps[0, 0], leg_maps[1, 0])
    grad_leg = (leg_maps[0, 1], leg_maps[1, 1])
    pol_leg = (leg_maps[0, 2], leg_maps[1, 2])
    three_leg = (leg_maps[0, 3], leg_maps[1, 3])
    one_leg = (leg_maps[0, 4], leg_maps[1, 4])
    temp_term = complex_mul(temp_leg, grad_leg)
    raise_term = conj_mul(pol_leg, three_leg)
    lower_term = conj_mul(one_leg, pol_leg)
    current = (
        temp_term[0] + 0.5 * (raise_term[0] + lower_term[0]),
        temp_term[1] + 0.5 * (raise_term[1] + lower_term[1]),
    )
    current_rows = jnp.stack(row_transform((current[0][None], current[1][None]), -1.0))
    current_modes = to_frequency(current_rows)
    out_weight = mask_out * response
    estimate_modes = complex_mul(
        lowering, (out_weight * current_modes[0, 0], out_weight * current_modes[1, 0])
    )
    estimate_stack = jnp.stack([estimate_modes[0][None], estimate_modes[1][None]])
    estimate_maps = to_space(inverse_columns(estimate_stack))
    slab_result = estimate_maps[:, 0]
    return lax.all_to_all(slab_result, "rows", split_axis=1, concat_axis=2, tiled=True)


def solution(mesh):
    placed = (
        P("sims", "rows", "fields"),
        P(),
        P(None, ("rows", "fields"), None),
        P(None, ("rows", "fields"), None),
        P(("rows", "fields"), None),
    )
    return jax.shard_map(
        body, mesh=mesh, in_specs=placed, out_specs=P("sims", "rows", "fields"), check_vma=False
    )
```

profile of v0, /device:TPU:1, one launch (start us, length us, event | category | flops | bytes accessed | tf_op | source)
XLA Modules:
  0.0 571.0 jit_solution(2138556085943826780)
XLA Ops:
  0.0 6.7 %copy.84 = f32[3,8,4096]{1,0,2:T(4,128)} copy(f32[3,8,4096]{2,1,0:T(8,128)} %param.5) | data formatting | bytes 786432 | tf_op args[0]
  6.7 7.5 %reshape.1834 = f32[4,1,24576]{2,1,0:T(1,128)} reshape(f32[4096,3,8]{2,1,0:T(4,128)} %bitcast.453) | data formatting | bytes 786432
  14.2 4.3 all-to-all-start
  18.5 6.2 %all-to-all-done = f32[4,1,24576]{2,1,0:T(1,128)S(1)} async-done(((f32[4,1,24576]{2,1,0:T(1,128)}), f32[4,1,24576]{2,1,0:T(1,128)S(1)}, u32[]{:S(2)}, u32[]{:S(2)}) %all-to-all-start) | async-done | bytes 393248 | tf_op jit(solution)/shard_map/all_to_all | solution.py:177
  25.3 1.8 reduce
  27.0 8.7 %reshape.1835 = f32[4096,3,8]{2,1,0:T(4,128)} reshape(f32[4,24576]{1,0:T(4,128)S(1)} %reduce) | data formatting | bytes 786432
  35.8 6.9 %copy.170 = f32[3,8,4,1024]{3,2,1,0:T(4,128)S(1)} copy(f32[3,8,4,1024]{1,0,3,2:T(4,128)} %bitcast.452) | data formatting | bytes 786432 | tf_op jit(solution)/shard_map/all_to_all | solution.py:177
  49.0 14.1 %all_to_all.165 = f32[2,3,4,4,2,1,1,1024]{7,4,3,1,6,5,0,2:T(2,128)S(1)} all-to-all(f32[2,3,4,4,2,1,1,1024]{7,4,3,1,6,5,0,2:T(2,128)S(1)} %copy.92), channel_id=1, replica_groups=mesh['sims'=2,'rows'=4,'fields'=4] {'rows'}, dimensions={2} | all-to-all | bytes 1572864 | tf_op jit(solution)/shard_map/all_to_all | solution.py:150
  64.1 5.4 all-to-all-start.2
  77.4 11.7 %all-to-all-done.2 = f32[2,3,1,4,2,4,1,1024]{7,4,5,1,0,6,2,3:T(2,128)S(1)} async-done(((f32[2,3,1,4,2,4,1,1024]{7,4,5,1,0,6,2,3:T(2,128)}), f32[2,3,1,4,2,4,1,1024]{7,4,5,1,0,6,2,3:T(2,128)S(1)}, u32[]{:S(2)}, u32[]{:S(2)}) %all-to-all-start.2) | async-done | bytes 786464 | tf_op jit(solution)/shard_map/all_to_all | solution.py:149
  92.2 18.6 %fusion.24 = f32[1024,3,2,16]{0,3,2,1:T(8,128)S(1)} fusion(f32[16,3,2,1024]{3,0,2,1:T(8,128)S(1)} %convolution_add_fusion.3, f32[16,3,2,1024]{3,0,2,1:T(8,128)S(1)} %convolution_subtract_fusion.3, f32[16,1024]{1,0:T(8,128)S(1)} %get-tuple-element.50, f32[16,1024]{1,0:T(8,128)S(1)} %get-tuple-element.51), kind=kOutput, calls=%fused_computation.27 | convolution fusion | flops 1222934528 | bytes 1310720 | tf_op jit(solution)/shard_map/brkc,cq->brqk/dot_general | solution.py:31
  110.8 19.3 %fusion.22 = f32[1024,3,2,16]{0,3,2,1:T(8,128)} fusion(f32[16,3,2,1024]{3,0,2,1:T(8,128)S(1)} %convolution_add_fusion.3, f32[16,3,2,1024]{3,0,2,1:T(8,128)S(1)} %convolution_subtract_fusion.3, f32[16,1024]{1,0:T(8,128)S(1)} %get-tuple-element.50, f32[16,1024]{1,0:T(8,128)S(1)} %get-tuple-element.51), kind=kOutput, calls=%fused_computation.25 | convolution fusion | flops 1222934528 | bytes 1310720 | tf_op jit(solution)/shard_map/brkc,cq->brqk/dot_general | solution.py:35
  130.0 19.2 %fusion.88 = f32[3,2,1024,16]{2,3,1,0:T(8,128)} fusion(f32[1024,3,2,16]{0,3,2,1:T(8,128)S(1)} %fusion.24, f32[16,3,2,1024]{3,0,2,1:T(8,128)S(1)} %convolution_add_fusion.3, f32[16,3,2,1024]{3,0,2,1:T(8,128)S(1)} %convolution_subtract_fusion.3, f32[16,1024]{1,0:T(8,128)S(1)} %get-tuple-element.50, f32[16,1024]{1,0:T(8,128)S(1)} %get-tuple-element.51), kind=kOutput, calls=%fused_computation.84 | convolution fusion | flops 1223032832 | bytes 1703936 | tf_op jit(solution)/shard_map/brkc,cq->brqk/dot_general | solution.py:34
  149.3 1.9 copy.96
  151.2 2.5 stack_reshape.4
  153.6 20.8 %fusion.94 = f32[3,2,1024,16]{2,3,1,0:T(8,128)} fusion(f32[1024,3,2,16]{0,3,2,1:T(8,128)} %fusion.22, f32[16,3,2,1024]{3,0,2,1:T(8,128)} %copy-done.6, f32[16,3,2,1024]{3,0,2,1:T(8,128)} %copy-done.5, f32[16,1024]{1,0:T(8,128)} %copy-done.8, f32[16,1024]{1,0:T(8,128)} %copy-done.10), kind=kOutput, calls=%fused_computation.86 | convolution fusion | flops 1223032832 | bytes 1703936 | tf_op jit(solution)/shard_map/brkc,cq->brqk/dot_general | solution.py:32
  174.5 1.9 copy.97
  176.4 2.4 stack_reshape.5
  178.8 2.9 fusion.150
  181.7 1.3 fusion.152
  185.1 1.5 subtract_negate_fusion.1
  187.8 1.3 fusion.153
  189.8 1.3 stack.74
  194.0 20.3 %fusion.16 = f32[5,2,16,1024]{3,2,1,0:T(8,128)} fusion(f32[5,2,1024,16]{2,3,1,0:T(8,128)} %constant_dynamic-update-slice_fusion), kind=kOutput, calls=%fused_computation.19 | convolution fusion | flops 2027945984 | bytes 1310720 | tf_op jit(solution)/shard_map/brqk,qc->brkc/dot_general | solution.py:31
  218.4 18.7 %fusion.14 = f32[5,2,16,1024]{3,2,1,0:T(8,128)S(1)} fusion(f32[5,2,1024,16]{2,3,1,0:T(8,128)S(1)} %constant_dynamic-update-slice_fusion.5), kind=kOutput, calls=%fused_computation.17 | convolution fusion | flops 2027945984 | bytes 1310720 | tf_op jit(solution)/shard_map/brqk,qc->brkc/dot_general | solution.py:35
  237.1 20.2 %fusion.77 = f32[5,2,16,1024]{3,2,1,0:T(8,128)S(1)} fusion(f32[5,2,16,1024]{3,2,1,0:T(8,128)S(1)} %copy-done.19, f32[5,2,1024,16]{2,3,1,0:T(8,128)} %copy-done.13), kind=kOutput, calls=%fused_computation.75 | convolution fusion | flops 2028109824 | bytes 1966080 | tf_op jit(solution)/shard_map/brqk,qc->brkc/dot_general | solution.py:34
  257.4 18.8 %fusion.80 = f32[5,2,16,1024]{3,2,1,0:T(8,128)S(1)} fusion(f32[5,2,16,1024]{3,2,1,0:T(8,128)S(1)} %fusion.14, f32[5,2,1024,16]{2,3,1,0:T(8,128)S(1)} %copy-done.12), kind=kOutput, calls=%fused_computation.76 | convolution fusion | flops 2028109824 | bytes 1966080 | tf_op jit(solution)/shard_map/brqk,qc->brkc/dot_general | solution.py:32
  280.2 20.0 %all_to_all.166 = f32[2,5,1,1,2,4,4,1024]{7,6,4,1,3,2,0,5:T(4,128)S(1)} all-to-all(f32[2,5,1,1,2,4,4,1024]{7,6,4,1,3,2,0,5:T(4,128)S(1)} %copy.171), channel_id=1, replica_groups=mesh['sims'=2,'rows'=4,'fields'=4] {'rows'}, dimensions={5} | all-to-all | bytes 2621440 | tf_op jit(solution)/shard_map/all_to_all | solution.py:166
  300.2 2.0 copy.110
  302.2 3.7 all-to-all-start.4
  306.0 30.6 %all-to-all-done.4 = f32[2,5,4,1,2,1,4,1024]{7,2,4,1,0,5,3,6:T(4,128)S(1)} async-done(((f32[2,5,4,1,2,1,4,1024]{7,2,4,1,0,5,3,6:T(4,128)}), f32[2,5,4,1,2,1,4,1024]{7,2,4,1,0,5,3,6:T(4,128)S(1)}, u32[]{:S(2)}, u32[]{:S(2)}) %all-to-all-start.4) | async-done | bytes 1310752 | tf_op jit(solution)/shard_map/all_to_all | solution.py:165
  336.8 1.2 fusion.282
  339.3 1.3 convolution_add_fusion.2
  340.6 1.5 add_bitcast_fusion
  351.8 8.8 %all_to_all.167 = f32[2,1,4,4,2,1,1,1024]{7,4,3,6,5,1,0,2:T(2,128)S(1)} all-to-all(f32[2,1,4,4,2,1,1,1024]{7,4,3,6,5,1,0,2:T(2,128)S(1)} %copy.129), channel_id=1, replica_groups=mesh['sims'=2,'rows'=4,'fields'=4] {'rows'}, dimensions={2} | all-to-all | bytes 524288 | tf_op jit(solution)/shard_map/all_to_all | solution.py:150
  361.3 3.4 all-to-all-start.6
  367.1 5.1 all-to-all-done.6
  373.8 18.3 %fusion.12 = f32[1024,2,16]{0,2,1:T(8,128)S(1)} fusion(f32[16,1,2,1024]{3,0,2,1:T(8,128)S(1)} %fusion.97, f32[16,1,2,1024]{3,0,2,1:T(8,128)S(1)} %fusion.98, f32[16,1024]{1,0:T(8,128)S(1)} %copy-done.9, f32[16,1024]{1,0:T(8,128)S(1)} %copy-done.11), kind=kOutput, calls=%fused_computation.15 | convolution fusion | flops 417431552 | bytes 524288 | tf_op jit(solution)/shard_map/brkc,cq->brqk/dot_general | solution.py:34
  392.2 18.3 %fusion.10 = f32[1024,2,16]{0,2,1:T(8,128)S(1)} fusion(f32[16,1,2,1024]{3,0,2,1:T(8,128)S(1)} %fusion.97, f32[16,1,2,1024]{3,0,2,1:T(8,128)S(1)} %fusion.98, f32[16,1024]{1,0:T(8,128)S(1)} %copy-done.9, f32[16,1024]{1,0:T(8,128)S(1)} %copy-done.11), kind=kOutput, calls=%fused_computation.13 | convolution fusion | flops 417431552 | bytes 524288 | tf_op jit(solution)/shard_map/brkc,cq->brqk/dot_general | solution.py:32
  410.5 18.4 %fusion.114 = f32[1,2,1024,16]{2,3,1,0:T(8,128)S(1)} fusion(f32[1024,2,16]{0,2,1:T(8,128)S(1)} %fusion.12, f32[16,1,2,1024]{3,0,2,1:T(8,128)S(1)} %fusion.97, f32[16,1,2,1024]{3,0,2,1:T(8,128)S(1)} %fusion.98, f32[16,1024]{1,0:T(8,128)S(1)} %copy-done.9, f32[16,1024]{1,0:T(8,128)S(1)} %copy-done.11), kind=kOutput, calls=%fused_computation.110 | convolution fusion | flops 417464320 | bytes 655360 | tf_op jit(solution)/shard_map/brkc,cq->brqk/dot_general | solution.py:31
  429.8 18.2 %fusion.120 = f32[1,2,1024,16]{2,3,1,0:T(8,128)S(1)} fusion(f32[1024,2,16]{0,2,1:T(8,128)S(1)} %fusion.10, f32[16,1,2,1024]{3,0,2,1:T(8,128)S(1)} %fusion.97, f32[16,1,2,1024]{3,0,2,1:T(8,128)S(1)} %fusion.98, f32[16,1024]{1,0:T(8,128)S(1)} %copy-done.9, f32[16,1024]{1,0:T(8,128)S(1)} %copy-done.11), kind=kOutput, calls=%fused_computation.112 | convolution fusion | flops 417464320 | bytes 655360 | tf_op jit(solution)/shard_map/brkc,cq->brqk/dot_general | solution.py:35
  449.7 21.4 %fusion.4 = f32[2,16,1024]{2,1,0:T(8,128)S(1)} fusion(f32[2,1024,16]{2,1,0:T(8,128)S(1)} %reshape.1797), kind=kOutput, calls=%fused_computation.7 | convolution fusion | flops 417333248 | bytes 262144 | tf_op jit(solution)/shard_map/brqk,qc->brkc/dot_general | solution.py:34
  471.5 21.2 %fusion.2 = f32[2,16,1024]{2,1,0:T(8,128)S(1)} fusion(f32[2,1024,16]{2,1,0:T(8,128)S(1)} %reshape.1796), kind=kOutput, calls=%fused_computation.5 | convolution fusion | flops 417333248 | bytes 262144 | tf_op jit(solution)/shard_map/brqk,qc->brkc/dot_general | solution.py:32
  492.6 21.5 %fusion.105 = f32[2,16,1024]{2,1,0:T(8,128)S(1)} fusion(f32[2,16,1024]{2,1,0:T(8,128)S(1)} %fusion.4, f32[2,1024,16]{2,1,0:T(8,128)S(1)} %reshape.1796), kind=kOutput, calls=%fused_computation.107 | convolution fusion | flops 417366016 | bytes 393216 | tf_op jit(solution)/shard_map/brqk,qc->brkc/dot_general | solution.py:31
  514.1 21.1 %fusion.108 = f32[2,16,1024]{2,1,0:T(8,128)S(1)} fusion(f32[2,16,1024]{2,1,0:T(8,128)S(1)} %fusion.2, f32[2,1024,16]{2,1,0:T(8,128)S(1)} %reshape.1797), kind=kOutput, calls=%fused_computation.108 | convolution fusion | flops 417366016 | bytes 393216 | tf_op jit(solution)/shard_map/brqk,qc->brkc/dot_general | solution.py:35
  536.9 9.6 %all_to_all.168 = f32[2,1,1,1,2,4,4,1024]{7,6,4,3,2,1,0,5:T(4,128)S(1)} all-to-all(f32[2,1,1,1,2,4,4,1024]{7,6,4,3,2,1,0,5:T(4,128)S(1)} %copy.172), channel_id=1, replica_groups=mesh['sims'=2,'rows'=4,'fields'=4] {'rows'}, dimensions={5} | all-to-all | bytes 524288 | tf_op jit(solution)/shard_map/all_to_all | solution.py:166
  546.7 9.1 %all_to_all.169 = f32[2,1,4,1,2,1,4,1024]{7,2,4,0,5,3,1,6:T(4,128)S(1)} all-to-all(f32[2,1,4,1,2,1,4,1024]{7,2,4,0,5,3,1,6:T(4,128)S(1)} %copy.141), channel_id=1, replica_groups=mesh['sims'=2,'rows'=4,'fields'=4] {'fields'}, dimensions={6} | all-to-all | bytes 524288 | tf_op jit(solution)/shard_map/all_to_all | solution.py:165
  559.4 10.6 %all_to_all.170 = f32[2,32,1024]{2,0,1:T(2,128)S(1)} all-to-all(f32[2,32,1024]{2,0,1:T(2,128)S(1)} %copy.148), channel_id=1, replica_groups=mesh['sims'=2,'rows'=4,'fields'=4] {'rows'}, dimensions={1} | all-to-all | bytes 524288 | tf_op jit(solution)/shard_map/all_to_all | solution.py:257
  (181 shorter events, 50.5 us)
Async XLA Ops:
  14.2 10.6 %all-to-all-start = ((f32[4,1,24576]{2,1,0:T(1,128)}), f32[4,1,24576]{2,1,0:T(1,128)S(1)}, u32[]{:S(2)}, u32[]{:S(2)}) async-start(f32[4,1,24576]{2,1,0:T(1,128)} %reshape.1834), calls=%async_computation | async-start | bytes 786432 | tf_op jit(solution)/shard_map/all_to_all | solution.py:177
  48.0 21.5 %copy-start.14 = (s32[6]{0:T(128)S(1)}, s32[6]{0:T(128)}, u32[]{:S(2)}) copy-start(s32[6]{0:T(128)} %param.6) | copy-start | bytes 76
  64.1 25.1 %all-to-all-start.2 = ((f32[2,3,1,4,2,4,1,1024]{7,4,5,1,0,6,2,3:T(2,128)}), f32[2,3,1,4,2,4,1,1024]{7,4,5,1,0,6,2,3:T(2,128)S(1)}, u32[]{:S(2)}, u32[]{:S(2)}) async-start(f32[2,3,1,4,2,4,1,1024]{7,4,5,1,0,6,2,3:T(2,128)} %copy.93), calls=%async_computation.2 | async-start | bytes 1572864 | tf_op jit(solution)/shard_map/all_to_all | solution.py:149
  77.1 52.9 %copy-start.8 = (f32[16,1024]{1,0:T(8,128)}, f32[16,1024]{1,0:T(8,128)S(1)}, u32[]{:S(2)}) copy-start(f32[16,1024]{1,0:T(8,128)S(1)} %get-tuple-element.50) | copy-start | bytes 196612
  77.1 52.9 %copy-start.10 = (f32[16,1024]{1,0:T(8,128)}, f32[16,1024]{1,0:T(8,128)S(1)}, u32[]{:S(2)}) copy-start(f32[16,1024]{1,0:T(8,128)S(1)} %get-tuple-element.51) | copy-start | bytes 196612
  77.4 107.6 %copy-start.2 = (s32[16384]{0:T(1024)}, s32[16384]{0:T(1024)S(1)}, u32[]{:S(2)}) copy-start(s32[16384]{0:T(1024)S(1)} %get-tuple-element.54) | copy-start | bytes 196612
  91.7 38.4 %copy-start.5 = (f32[16,3,2,1024]{3,0,2,1:T(8,128)}, f32[16,3,2,1024]{3,0,2,1:T(8,128)S(1)}, u32[]{:S(2)}) copy-start(f32[16,3,2,1024]{3,0,2,1:T(8,128)S(1)} %convolution_subtract_fusion.3) | copy-start | bytes 1179652
  92.2 37.8 %copy-start.6 = (f32[16,3,2,1024]{3,0,2,1:T(8,128)}, f32[16,3,2,1024]{3,0,2,1:T(8,128)S(1)}, u32[]{:S(2)}) copy-start(f32[16,3,2,1024]{3,0,2,1:T(8,128)S(1)} %convolution_add_fusion.3) | copy-start | bytes 1179652
  178.8 6.2 %copy-start = (f32[1,3,2,16384]{3,2,1,0:T(2,128)S(1)}, f32[1,3,2,16384]{3,2,1,0:T(2,128)}, u32[]{:S(2)}) copy-start(f32[1,3,2,16384]{3,2,1,0:T(2,128)} %stack_reshape.4) | copy-start | bytes 1179652
  178.8 6.2 %copy-start.1 = (f32[1,3,2,16384]{3,2,1,0:T(2,128)S(1)}, f32[1,3,2,16384]{3,2,1,0:T(2,128)}, u32[]{:S(2)}) copy-start(f32[1,3,2,16384]{3,2,1,0:T(2,128)} %stack_reshape.5) | copy-start | bytes 1179652
  178.8 6.3 %copy-start.15 = (s32[2]{0:T(128)S(1)}, s32[2]{0:T(128)}, u32[]{:S(2)}) copy-start(s32[2]{0:T(128)} %get-tuple-element.47) | copy-start | bytes 28
  178.8 6.3 %copy-start.18 = (s32[2]{0:T(128)S(1)}, s32[2]{0:T(128)}, u32[]{:S(2)}) copy-start(s32[2]{0:T(128)} %get-tuple-element.46) | copy-start | bytes 28
  183.4 4.4 copy-start.4
  217.6 0.8 copy-start.13
  218.4 18.7 %copy-start.19 = (f32[5,2,16,1024]{3,2,1,0:T(8,128)S(1)}, f32[5,2,16,1024]{3,2,1,0:T(8,128)}, u32[]{:S(2)}) copy-start(f32[5,2,16,1024]{3,2,1,0:T(8,128)} %fusion.16) | copy-start | bytes 1966084
  237.1 20.3 %copy-start.12 = (f32[5,2,1024,16]{2,3,1,0:T(8,128)S(1)}, f32[5,2,1024,16]{2,3,1,0:T(8,128)}, u32[]{:S(2)}) copy-start(f32[5,2,1024,16]{2,3,1,0:T(8,128)} %constant_dynamic-update-slice_fusion) | copy-start | bytes 1966084
  302.2 34.4 %all-to-all-start.4 = ((f32[2,5,4,1,2,1,4,1024]{7,2,4,1,0,5,3,6:T(4,128)}), f32[2,5,4,1,2,1,4,1024]{7,2,4,1,0,5,3,6:T(4,128)S(1)}, u32[]{:S(2)}, u32[]{:S(2)}) async-start(f32[2,5,4,1,2,1,4,1024]{7,2,4,1,0,5,3,6:T(4,128)} %copy.110), calls=%async_computation.4 | async-start | bytes 2621440 | tf_op jit(solution)/shard_map/all_to_all | solution.py:165
  349.4 24.4 %copy-start.9 = (f32[16,1024]{1,0:T(8,128)S(1)}, f32[16,1024]{1,0:T(8,128)}, u32[]{:S(2)}) copy-start(f32[16,1024]{1,0:T(8,128)} %copy-done.8) | copy-start | bytes 196612
  349.4 24.4 %copy-start.11 = (f32[16,1024]{1,0:T(8,128)S(1)}, f32[16,1024]{1,0:T(8,128)}, u32[]{:S(2)}) copy-start(f32[16,1024]{1,0:T(8,128)} %copy-done.10) | copy-start | bytes 196612
  361.3 11.0 %all-to-all-start.6 = ((f32[2,1,1,4,2,4,1,1024]{7,4,5,0,6,2,1,3:T(2,128)}), f32[2,1,1,4,2,4,1,1024]{7,4,5,0,6,2,1,3:T(2,128)S(1)}, u32[]{:S(2)}, u32[]{:S(2)}) async-start(f32[2,1,1,4,2,4,1,1024]{7,4,5,0,6,2,1,3:T(2,128)} %copy.130), calls=%async_computation.6 | async-start | bytes 524288 | tf_op jit(solution)/shard_map/all_to_all | solution.py:149
  429.8 19.1 %copy-start.3 = (s32[16384]{0:T(1024)S(1)}, s32[16384]{0:T(1024)}, u32[]{:S(2)}) copy-start(s32[16384]{0:T(1024)} %copy-done.2) | copy-start | bytes 196612
  429.8 19.1 %copy-start.7 = (f32[2,16384]{1,0:T(2,128)S(1)}, f32[2,16384]{1,0:T(2,128)}, u32[]{:S(2)}) copy-start(f32[2,16384]{1,0:T(2,128)} %param.9) | copy-start | bytes 393220
  429.8 19.1 %copy-start.16 = (s32[2]{0:T(128)S(1)}, s32[2]{0:T(128)}, u32[]{:S(2)}) copy-start(s32[2]{0:T(128)} %get-tuple-element.47) | copy-start | bytes 28
  429.8 19.1 %copy-start.17 = (f32[2]{0:T(128)S(1)}, f32[2]{0:T(128)}, u32[]{:S(2)}) copy-start(f32[2]{0:T(128)} %get-tuple-element.45) | copy-start | bytes 28
where the time goes:
time: 579 us; the launch traced here: 571 us
  matrix products  342 us (59%)
  blocking collectives  72.3 us (12%)
  local copies, waits for them, and re-layouts  64.4 us (11%)
  waiting for transfers between devices  53.8 us (9%)
  starting transfers between devices  16.8 us (3%)
  other arithmetic  12.7 us (2%)
  between operations  8.9 us (2%)
    dot_general x16, matrix products, complex_einsum(): imag_out = jnp.einsum(formula, data_real, table_imag, precision=exact_mode)  86.3 us
    dot_general x15, matrix products, complex_einsum(): jnp.einsum(formula, data_imag, table_imag, precision=exact_mode)  86.3 us
    dot_general x16, matrix products, complex_einsum(): real_out = jnp.einsum(formula, data_real, table_real, precision=exact_mode)  85.9 us
    dot_general x15, matrix products, complex_einsum(): jnp.einsum(formula, data_imag, table_real, precision=exact_mode)  83.7 us
    all_to_all x1, waiting for transfers between devices, to_space(): lax.all_to_all(lax.all_to_all(shaped, 'rows', split_axis=5, concat_axis=2...  30.6 us
    all_to_all x2, blocking collectives, to_space(): lax.all_to_all(shaped, 'rows', split_axis=5, concat_axis=2, tiled=True)  29.7 us
    unnamed x51, local copies, waits for them, and re-layouts  26.6 us
    all_to_all x2, blocking collectives, to_frequency(): lax.all_to_all(shaped, 'rows', split_axis=2, concat_axis=5, tiled=True)  22.9 us
  transfers between devices with their start and end apart: 4, of which 4 were waited for; matrix products, arithmetic and copies ran while one was open for 1% of the time, Pallas kernels for 0%

commit v1 on v0

--- a/solution.py
+++ b/solution.py
@@ -1,8 +1,12 @@
+import functools
 import math
 
 import jax
 import jax.numpy as jnp
+import numpy as np
 from jax import lax
+from jax.experimental import pallas as pl
+from jax.experimental.pallas import tpu as pltpu
 from jax.sharding import PartitionSpec as P
 
 NC = 16384
@@ -257,6 +261,464 @@
     return lax.all_to_all(slab_result, "rows", split_axis=1, concat_axis=2, tiled=True)
 
 
+SIDE = 128
+TILE = (8, 128)
+MESH = pl.DeviceIdType.MESH
+
+
+def add_pair(a, b):
+    imag = a[1] if b[1] is None else b[1] if a[1] is None else a[1] + b[1]
+    return (a[0] + b[0], imag)
+
+
+def sub_pair(a, b):
+    imag = a[1] if b[1] is None else -b[1] if a[1] is None else a[1] - b[1]
+    return (a[0] - b[0], imag)
+
+
+def turn_pair(value, step, length, direction):
+    real, imag = value
+    if step == 0:
+        return value
+    if 4 * step == length:
+        if imag is None:
+            return (jnp.zeros_like(real), real if direction > 0 else -real)
+        return (-imag, real) if direction > 0 else (imag, -real)
+    angle = 2.0 * math.pi * step / length
+    c, s = math.cos(angle), direction * math.sin(angle)
+    if imag is None:
+        return (real * c, real * s)
+    if 8 * step == length:
+        if direction > 0:
+            return ((real - imag) * c, (real + imag) * c)
+        return ((real + imag) * c, (imag - real) * c)
+    if 8 * step == 3 * length:
+        if direction > 0:
+            return ((real + imag) * c, (imag - real) * c)
+        return ((real - imag) * c, (real + imag) * c)
+    return (real * c - imag * s, real * s + imag * c)
+
+
+def short_transform(values, direction):
+    length = len(values)
+    if length == 1:
+        return values
+    even = short_transform(values[0::2], direction)
+    odd = short_transform(values[1::2], direction)
+    low, high = [], []
+    for step in range(length // 2):
+        turned = turn_pair(odd[step], step, length, direction)
+        low.append(add_pair(even[step], turned))
+        high.append(sub_pair(even[step], turned))
+    return low + high
+
+
+def split_number(x):
+    top = x.astype(jnp.bfloat16)
+    return top, (x - top.astype(jnp.float32)).astype(jnp.bfloat16)
+
+
+def dot32(a, b):
+    return jnp.dot(a, b, preferred_element_type=jnp.float32)
+
+
+def matrix_left(table_ref, which, x):
+    top, rest = split_number(x)
+    m_top, m_rest = table_ref[which, 0], table_ref[which, 1]
+    return dot32(m_top, top) + (dot32(m_top, rest) + dot32(m_rest, top))
+
+
+def matrix_right(table_ref, which, x):
+    top, rest = split_number(x)
+    m_top, m_rest = table_ref[which, 0], table_ref[which, 1]
+    return dot32(top, m_top) + (dot32(top, m_rest) + dot32(rest, m_top))
+
+
+def lens_kernel(
+    rows_count, fields_count, local_rows,
+    cuts_ref, sky_ref, weight_ref, table_ref, twiddle_ref, out_ref,
+    slab_out, slab_in, spec_out, spec_in, weights, legs_out, legs_in, maps, current,
+    cur_out, cur_in, est_out, est_in, fin_out, fin_in,
+    slab_sem, spec_sem, legs_sem, cur_sem, est_sem, fin_sem, self_sem,
+):
+    groups = rows_count * fields_count
+    total_rows = groups * local_rows
+    in_rows = total_rows // rows_count
+    row_ratio = NC // total_rows
+    my_r, my_f = lax.axis_index("rows"), lax.axis_index("fields")
+    me = my_r * fields_count + my_f
+    my_block = my_f * rows_count + my_r
+
+    def place(index):
+        return index // fields_count, index % fields_count
+
+    def block_of(index):
+        r, f = place(index)
+        return f * rows_count + r
+
+    def target(index):
+        r, f = place(index)
+        return {"rows": r, "fields": f}
+
+    def send(q, src, dst, sems):
+        peer = (me + q) % groups
+        return pltpu.make_async_remote_copy(
+            src_ref=src, dst_ref=dst, send_sem=sems[0], recv_sem=sems[1],
+            device_id=target(peer), device_id_type=MESH,
+        )
+
+    def send_row(q, src, dst, sems):
+        return pltpu.make_async_remote_copy(
+            src_ref=src, dst_ref=dst, send_sem=sems[0], recv_sem=sems[1],
+            device_id={"rows": (my_r + q) % rows_count}, device_id_type=MESH,
+        )
+
+    def each_peer(body, count=groups):
+        def step(q, carry):
+            body(q)
+            return carry
+        lax.fori_loop(1, count, step, 0)
+
+    barrier = pltpu.get_barrier_semaphore()
+
+    def greet(q):
+        pl.semaphore_signal(
+            barrier, inc=1, device_id=target((me + q) % groups), device_id_type=MESH
+        )
+
+    each_peer(greet)
+    tiles = sky_ref.shape[2] // SIDE
+    for field in range(3):
+        for t in range(tiles):
+            slab_out[t // 8, field, :, t % 8, :] = sky_ref[field, :, t * SIDE:(t + 1) * SIDE]
+    pl.semaphore_wait(barrier, groups - 1)
+
+    def slab_copy(q):
+        return send_row(
+            q, slab_out.at[(my_r + q) % rows_count], slab_in.at[my_r],
+            (slab_sem.at[0, q], slab_sem.at[1, q]),
+        )
+
+    def slab_arrival(q):
+        return send_row(
+            q, slab_out.at[(my_r + q) % rows_count],
+            slab_in.at[(my_r + rows_count - q) % rows_count],
+            (slab_sem.at[0, q], slab_sem.at[1, q]),
+        )
+
+    each_peer(lambda q: slab_copy(q).start(), rows_count)
+    own = pltpu.make_async_copy(slab_out.at[my_r], slab_in.at[my_r], self_sem.at[0])
+    own.start()
+
+    low_index = lax.broadcasted_iota(jnp.int32, (SIDE, SIDE), 0)
+    high_index = lax.broadcasted_iota(jnp.int32, (SIDE, SIDE), 1)
+    column_ids = low_index + SIDE * high_index
+    freq_cols = jnp.where(column_ids < NC // 2, column_ids, column_ids - NC)
+
+    def row_frequency(row):
+        row_id = me * local_rows + row
+        return jnp.where(row_id < total_rows // 2, row_id, row_id - total_rows)
+
+    def weigh(row, carry):
+        scaled = row_ratio * row_frequency(row)
+        radius_sq = freq_cols * freq_cols + scaled * scaled
+
+        def mask(n):
+            low, high = cuts_ref[2 * n], cuts_ref[2 * n + 1]
+            inside = (radius_sq >= low * low) & (radius_sq <= high * high)
+            return inside.astype(jnp.float32)
+
+        pol = mask(1)
+        weights[0, row] = mask(0) * weight_ref[0, row].T
+        weights[1, row] = pol * weight_ref[1, row].T
+        weights[2, row] = pol * weight_ref[2, row].T
+        weights[3, row] = weight_ref[3, row].T
+        weights[4, row] = weight_ref[4, row].T
+        weights[5, row] = mask(2) * weight_ref[5, row].T
+        return carry
+
+    lax.fori_loop(0, local_rows, weigh, 0)
+
+    each_peer(lambda q: slab_arrival(q).wait_recv(), rows_count)
+    own.wait()
+
+    def spec_copy(field, q, src_block):
+        peer = (me + q) % groups
+        return send(
+            q, spec_out.at[field, peer], spec_in.at[field, :, :, src_block],
+            (spec_sem.at[0, field, q], spec_sem.at[1, field, q]),
+        )
+
+    def own_spec(field):
+        return pltpu.make_async_copy(
+            spec_out.at[field, me], spec_in.at[field, :, :, my_block], self_sem.at[1 + field]
+        )
+
+    def row_step(field, carry):
+        values = [
+            (slab_in[y // in_rows, field, y % in_rows], None) for y in range(total_rows)
+        ]
+        for k, (real, imag) in enumerate(short_transform(values, -1)):
+            spec_out[field, k // local_rows, k % local_rows, 0] = real
+            spec_out[field, k // local_rows, k % local_rows, 1] = (
+                jnp.zeros_like(real) if imag is None else imag
+            )
+        each_peer(lambda q: spec_copy(field, q, my_block).start())
+        own_spec(field).start()
+        return carry
+
+    lax.fori_loop(0, 3, row_step, 0)
+
+    def row_wait(field, carry):
+        each_peer(
+            lambda q: spec_copy(field, q, block_of((me + groups - q) % groups)).wait_recv()
+        )
+        own_spec(field).wait()
+        return carry
+
+    lax.fori_loop(0, 3, row_wait, 0)
+
+    cos_f, sin_f, cos_b, sin_b = 0, 1, 2, 3
+
+    def long_forward(pieces):
+        turned = []
+        for piece in pieces:
+            y = matrix_left(table_ref, 0, piece)
+            yr, yi = y[:SIDE], y[SIDE:]
+            c, s = twiddle_ref[cos_f], twiddle_ref[sin_f]
+            z = jnp.concatenate([yr * c - yi * s, yr * s + yi * c], axis=1)
+            z = matrix_right(table_ref, 1, z)
+            turned.append((z[:, :SIDE], z[:, SIDE:]))
+        return turned
+
+    def long_inverse(pair):
+        u = matrix_right(table_ref, 0, jnp.concatenate([pair[0], pair[1]], axis=1))
+        ur, ui = u[:, :SIDE], u[:, SIDE:]
+        c, s = twiddle_ref[cos_b], twiddle_ref[sin_b]
+        v = jnp.concatenate([ur * c - ui * s, ur * s + ui * c], axis=0)
+        return matrix_left(table_ref, 1, v)
+
+    def legs_copy(row, q, src_index):
+        peer = (me + q) % groups
+        return send(
+            q, legs_out.at[row, :, :, block_of(peer)], legs_in.at[row, src_index],
+            (legs_sem.at[0, row, q], legs_sem.at[1, row, q]),
+        )
+
+    def own_legs(row):
+        return pltpu.make_async_copy(
+            legs_out.at[row, :, :, my_block], legs_in.at[row, me], self_sem.at[4 + row]
+        )
+
+    def slopes(row):
+        along_x = (2 * freq_cols).astype(jnp.float32) / NC
+        along_y = (2 * row_frequency(row)).astype(jnp.float32) / total_rows
+        return along_x, along_y
+
+    def leg_step(row, carry):
+        temp, stokes_q, stokes_u = long_forward(
+            [spec_in[field, row].reshape(2 * SIDE, SIDE) for field in range(3)]
+        )
+        scaled = row_ratio * row_frequency(row)
+        radius_sq = freq_cols * freq_cols + scaled * scaled
+        floor = jnp.maximum(radius_sq, 1).astype(jnp.float32)
+        cos2 = (freq_cols * freq_cols - scaled * scaled).astype(jnp.float32) / floor
+        sin2 = (2 * freq_cols * scaled).astype(jnp.float32) / floor
+        along_x, along_y = slopes(row)
+        raising, lowering = (-along_y, along_x), (along_y, along_x)
+        rot = (cos2, sin2)
+        w_t, w_e, w_b = weights[0, row], weights[1, row], weights[2, row]
+        w_gt, w_ge = weights[3, row], weights[4, row]
+        t_bar = (w_t * temp[0], w_t * temp[1])
+        e_bar = tuple(-w_e * (cos2 * a + sin2 * b) for a, b in zip(stokes_q, stokes_u))
+        b_bar = tuple(w_b * (sin2 * a - cos2 * b) for a, b in zip(stokes_q, stokes_u))
+        g = complex_mul((w_gt * t_bar[0], w_gt * t_bar[1]), raising)
+        p = complex_mul((b_bar[1] - e_bar[0], -(e_bar[1] + b_bar[0])), rot)
+        w = complex_mul((-w_ge * e_bar[0], -w_ge * e_bar[1]), rot)
+        h3 = complex_mul(w, raising)
+        h1 = complex_mul(w, lowering)
+        for n, leg in enumerate((t_bar, g, p, h3, h1)):
+            legs_out[row, n] = long_inverse(leg).reshape((2, groups) + TILE)
+        each_peer(lambda q: legs_copy(row, q, me).start())
+        own_legs(row).start()
+        return carry
+
+    lax.fori_loop(0, local_rows, leg_step, 0)
+
+    def leg_wait(row, carry):
+        each_peer(lambda q: legs_copy(row, q, (me + groups - q) % groups).wait_recv())
+        own_legs(row).wait()
+        return carry
+
+    lax.fori_loop(0, local_rows, leg_wait, 0)
+
+    def map_step(n, carry):
+        values = [
+            (legs_in[k % local_rows, k // local_rows, n, 0],
+             legs_in[k % local_rows, k // local_rows, n, 1])
+            for k in range(total_rows)
+        ]
+        for y, (real, imag) in enumerate(short_transform(values, 1)):
+            maps[n, 0, y] = real
+            maps[n, 1, y] = imag
+        return carry
+
+    lax.fori_loop(0, 5, map_step, 0)
+
+    def product_step(y, carry):
+        a, g, p, h3, h1 = [(maps[n, 0, y], maps[n, 1, y]) for n in range(5)]
+        ag, ph, hp = complex_mul(a, g), conj_mul(p, h3), conj_mul(h1, p)
+        current[0, y] = ag[0] + 0.5 * (ph[0] + hp[0])
+        current[1, y] = ag[1] + 0.5 * (ph[1] + hp[1])
+        return carry
+
+    lax.fori_loop(0, total_rows, product_step, 0)
+
+    values = [(current[0, y], current[1, y]) for y in range(total_rows)]
+    for k, (real, imag) in enumerate(short_transform(values, -1)):
+        cur_out[k // local_rows, k % local_rows, 0] = real
+        cur_out[k // local_rows, k % local_rows, 1] = imag
+
+    def cur_copy(q, src_block):
+        return send(
+            q, cur_out.at[(me + q) % groups], cur_in.at[:, :, src_block],
+            (cur_sem.at[0, q], cur_sem.at[1, q]),
+        )
+
+    each_peer(lambda q: cur_copy(q, my_block).start())
+    own_cur = pltpu.make_async_copy(
+        cur_out.at[me], cur_in.at[:, :, my_block], self_sem.at[4 + local_rows]
+    )
+    own_cur.start()
+    each_peer(lambda q: cur_copy(q, block_of((me + groups - q) % groups)).wait_recv())
+    own_cur.wait()
+
+    def estimate_step(row, carry):
+        (modes,) = long_forward([cur_in[row].reshape(2 * SIDE, SIDE)])
+        along_x, along_y = slopes(row)
+        w = weights[5, row]
+        estimate = complex_mul((w * modes[0], w * modes[1]), (along_y, along_x))
+        est_out[row] = long_inverse(estimate).reshape((2, groups) + TILE)
+        return carry
+
+    lax.fori_loop(0, local_rows, estimate_step, 0)
+
+    def est_copy(q, src_index):
+        return send(
+            q, est_out.at[:, :, block_of((me + q) % groups)], est_in.at[src_index],
+            (est_sem.at[0, q], est_sem.at[1, q]),
+        )
+
+    each_peer(lambda q: est_copy(q, me).start())
+    own_est = pltpu.make_async_copy(
+        est_out.at[:, :, my_block], est_in.at[me], self_sem.at[5 + local_rows]
+    )
+    own_est.start()
+    each_peer(lambda q: est_copy(q, (me + groups - q) % groups).wait_recv())
+    own_est.wait()
+
+    values = [
+        (est_in[k // local_rows, k % local_rows, 0], est_in[k // local_rows, k % local_rows, 1])
+        for k in range(total_rows)
+    ]
+    for y, (real, imag) in enumerate(short_transform(values, 1)):
+        fin_out[y // in_rows, 0, y % in_rows] = real
+        fin_out[y // in_rows, 1, y % in_rows] = imag
+
+    def fin_copy(q, src_row):
+        return send_row(
+            q, fin_out.at[(my_r + q) % rows_count], fin_in.at[src_row],
+            (fin_sem.at[0, q], fin_sem.at[1, q]),
+        )
+
+    each_peer(lambda q: fin_copy(q, my_r).start(), rows_count)
+    own_fin = pltpu.make_async_copy(
+        fin_out.at[my_r], fin_in.at[my_r], self_sem.at[6 + local_rows]
+    )
+    own_fin.start()
+    each_peer(
+        lambda q: fin_copy(q, (my_r + rows_count - q) % rows_count).wait_recv(), rows_count
+    )
+    own_fin.wait()
+    for part in range(2):
+        for t in range(tiles):
+            out_ref[part, :, t * SIDE:(t + 1) * SIDE] = fin_in[t // 8, part, :, t % 8, :]
+
+    each_peer(lambda q: slab_copy(q).wait_send(), rows_count)
+
+    def spec_left(field, carry):
+        each_peer(lambda q: spec_copy(field, q, my_block).wait_send())
+        return carry
+
+    lax.fori_loop(0, 3, spec_left, 0)
+
+    def legs_left(row, carry):
+        each_peer(lambda q: legs_copy(row, q, me).wait_send())
+        return carry
+
+    lax.fori_loop(0, local_rows, legs_left, 0)
+    each_peer(lambda q: cur_copy(q, my_block).wait_send())
+    each_peer(lambda q: est_copy(q, me).wait_send())
+    each_peer(lambda q: fin_copy(q, my_r).wait_send(), rows_count)
+
+
+def long_tables(total_rows):
+    index = np.arange(SIDE)
+    angle = 2.0 * np.pi * (index[:, None] * index[None, :] % SIDE) / SIDE
+    c, s = np.cos(angle), np.sin(angle)
+    forward = np.block([[c, s], [-s, c]]).astype(np.float32)
+    tables = np.stack([forward, forward.T])
+    top = tables.astype(jnp.bfloat16)
+    rest = (tables - top.astype(np.float32)).astype(jnp.bfloat16)
+    turn = 2.0 * np.pi * (index[:, None] * index[None, :]) / NC
+    scale = 1.0 / (NC * total_rows)
+    twiddle = np.stack(
+        [np.cos(turn), -np.sin(turn), scale * np.cos(turn), scale * np.sin(turn)]
+    ).astype(np.float32)
+    return np.stack([top, rest], axis=1), twiddle
+
+
+def fused_body(rows_count, fields_count, sky_maps, band_cuts, filters, wiener, response):
+    groups = rows_count * fields_count
+    local_rows = response.shape[0]
+    total_rows = local_rows * groups
+    in_rows = total_rows // rows_count
+    table, twiddle = long_tables(total_rows)
+    weight = jnp.concatenate([filters, wiener, response[None]]).reshape(
+        6, local_rows, SIDE, SIDE
+    )
+    vmem = pl.BlockSpec(memory_space=pltpu.VMEM)
+    f32 = jnp.float32
+    dma = pltpu.SemaphoreType.DMA
+    slab = pltpu.VMEM((rows_count, 3, in_rows) + TILE, f32)
+    chunk = pltpu.VMEM((groups, local_rows, 2) + TILE, f32)
+    lines = pltpu.VMEM((local_rows, 2, groups) + TILE, f32)
+    final = pltpu.VMEM((rows_count, 2, in_rows) + TILE, f32)
+    return pl.pallas_call(
+        functools.partial(lens_kernel, rows_count, fields_count, local_rows),
+        out_shape=jax.ShapeDtypeStruct((2,) + sky_maps.shape[1:], f32),
+        in_specs=[pl.BlockSpec(memory_space=pltpu.SMEM)] + [vmem] * 4,
+        out_specs=vmem,
+        scratch_shapes=[
+            slab, slab,
+            pltpu.VMEM((3, groups, local_rows, 2) + TILE, f32),
+            pltpu.VMEM((3, local_rows, 2, groups) + TILE, f32),
+            pltpu.VMEM((6, local_rows, SIDE, SIDE), f32),
+            pltpu.VMEM((local_rows, 5, 2, groups) + TILE, f32),
+            pltpu.VMEM((local_rows, groups, 5, 2) + TILE, f32),
+            pltpu.VMEM((5, 2, total_rows) + TILE, f32),
+            pltpu.VMEM((2, total_rows) + TILE, f32),
+            chunk, lines, lines, chunk, final, final,
+            dma((2, rows_count)), dma((2, 3, groups)), dma((2, local_rows, groups)),
+            dma((2, groups)), dma((2, groups)), dma((2, rows_count)), dma((7 + local_rows,)),
+        ],
+        compiler_params=pltpu.CompilerParams(
+            collective_id=0, has_side_effects=True, vmem_limit_bytes=48 * 1024 * 1024
+        ),
+        name="lens",
+    )(band_cuts, sky_maps, weight, jnp.asarray(table), jnp.asarray(twiddle))
+
+
 def solution(mesh):
     placed = (
         P("sims", "rows", "fields"),
@@ -265,6 +727,20 @@
         P(None, ("rows", "fields"), None),
         P(("rows", "fields"), None),
     )
+    rows_count, fields_count = mesh.shape["rows"], mesh.shape["fields"]
+    groups = rows_count * fields_count
+
+    def choose(sky_maps, *rest):
+        fits = (
+            NC == SIDE * SIDE
+            and NC // groups == TILE[0] * TILE[1]
+            and sky_maps.shape[1] % 8 == 0
+            and sky_maps.shape[1] * rows_count in (16, 32, 64)
+        )
+        if fits:
+            return fused_body(rows_count, fields_count, sky_maps, *rest)
+        return body(sky_maps, *rest)
+
     return jax.shard_map(
-        body, mesh=mesh, in_specs=placed, out_specs=P("sims", "rows", "fields"), check_vma=False
-    )
+        choose, mesh=mesh, in_specs=placed, out_specs=P("sims", "rows", "fields"), check_vma=False
+    )

time: 579 us -> 90.8 us (0.16); the launches traced: 571 us -> 90.7 us
  matrix products: 342 us -> 0 us
  Pallas kernels: 0 us -> 87.1 us
  blocking collectives: 72.3 us -> 0 us
  local copies, waits for them, and re-layouts: 64.4 us -> 3.42 us
  waiting for transfers between devices: 53.8 us -> 0 us
  starting transfers between devices: 16.8 us -> 0 us
  other arithmetic: 12.7 us -> 0.05 us
  between operations: 8.9 us -> 0.07 us
    dot_general x62 -> x0, matrix products: 342 us -> none  [the longest x16 86.3 us: complex_einsum(): imag_out = jnp.einsum(formula, data_real, table_imag, precision=exact_mode)]
    pallas_call x0 -> x1, Pallas kernels: none -> 87.1 us  [fused_body(): pl.pallas_call(functools.partial(lens_kernel, rows_count, fields_count, l...]
    all_to_all x6 -> x0, blocking collectives: 72.3 us -> none  [the longest x2 29.7 us: to_space(): lax.all_to_all(shaped, 'rows', split_axis=5, concat_axis=2, tiled=True)]
    all_to_all x4 -> x0, waiting for transfers between devices: 53.8 us -> none  [the longest x1 30.6 us: to_space(): lax.all_to_all(lax.all_to_all(shaped, 'rows', split_axis=5, concat_axis=2...]
    unnamed x51 -> x14, local copies, waits for them, and re-layouts: 26.6 us -> 2.86 us
    all_to_all x4 -> x0, starting transfers between devices: 16.8 us -> none  [the longest x2 8.81 us: to_frequency(): lax.all_to_all(lax.all_to_all(shaped, 'rows', split_axis=2, concat_axis=5...]
    another operation x40 -> x0, local copies, waits for them, and re-layouts: 16.7 us -> none  [the longest x11 5 us: body(): jnp.stack([temp_bar[0], grad_temp[0], pol_bar[0], spin_three[0], spin_one...]
    all_to_all x7 -> x0, local copies, waits for them, and re-layouts: 12.1 us -> none  [the longest x2 7.45 us: body(): lax.all_to_all(sky_maps, 'rows', split_axis=2, concat_axis=1, tiled=True)]
  transfers between devices with their start and end apart: 4 -> 0, of which waited for: 4 -> 0; matrix products, arithmetic and copies ran while one was open for 1% -> 0% of each run, Pallas kernels for 0% -> 0%
where the time goes in v1:
time: 90.8 us; the launch traced here: 90.7 us
  Pallas kernels  87.1 us (96%)
  local copies, waits for them, and re-layouts  3.42 us (4%)
    pallas_call x1, Pallas kernels, fused_body(): pl.pallas_call(functools.partial(lens_kernel, rows_count, fields_count, l...  87.1 us
    unnamed x14, local copies, waits for them, and re-layouts  2.86 us

profile of v1, /device:TPU:1, one launch (start us, length us, event | category | flops | bytes accessed | tf_op | source)
XLA Modules:
  0.0 90.7 jit_solution(9981596143997692273)
XLA Ops:
  0.0 0.0 copy-start.5
  0.0 0.0 copy-start.4
  0.0 1.0 %copy.10 = f32[1,2,128,128]{3,2,1,0:T(8,128)S(1)} copy(f32[1,2,128,128]{3,1,2,0:T(2,128)} %bitcast.5) | data formatting | bytes 262144
  1.0 0.0 copy-done.5
  1.0 0.2 concatenate.11
  1.2 0.0 copy-done.4
  1.3 0.3 concatenate.10
  1.6 0.0 copy-start
  1.6 0.0 copy-start.1
  1.6 0.0 copy-start.2
  1.6 0.0 copy-start.3
  1.6 0.1 pad_maximum_fusion.weight_ref
  1.7 0.9 %copy-done = bf16[2,2,256,256]{3,2,1,0:T(8,128)(2,1)S(1)} copy-done((bf16[2,2,256,256]{3,2,1,0:T(8,128)(2,1)S(1)}, bf16[2,2,256,256]{3,2,1,0:T(8,128)(2,1)}, u32[]{:S(2)}) %copy-start) | copy-done | bytes 524312
  2.6 0.1 copy-done.1
  2.8 0.1 copy-done.2
  2.8 0.0 copy-done.3
  2.8 87.1 %lens.1 = f32[2,8,4096]{2,1,0:T(8,128)S(1)} custom-call(s32[6]{0:T(128)S(1)} %copy-done.3, f32[3,8,4096]{2,1,0:T(8,128)S(1)} %copy-done.1, f32[6,2,128,128]{3,2,1,0:T(8,128)S(1)} %pad_maximum_fusion.weight_ref, bf16[2,2,256,256]{3,2,1,0:T(8,128)(2,1)S(1)} %copy-done, f32[4,128,128]{2,1,0:T(8,128)S(1)} %copy-done.2), custom_call_target="tpu_custom_call" | custom-call | tf_op jit(solution)/shard_map/lens/pallas_call | solution.py:697
  90.0 0.7 copy.12
Async XLA Ops:
  0.0 1.0 %copy-start.5 = (f32[2,2,16384]{2,1,0:T(2,128)S(1)}, f32[2,2,16384]{2,1,0:T(2,128)}, u32[]{:S(2)}) copy-start(f32[2,2,16384]{2,1,0:T(2,128)} %param.10) | copy-start | bytes 786436
  0.0 1.2 %copy-start.4 = (f32[3,2,16384]{2,1,0:T(2,128)S(1)}, f32[3,2,16384]{2,1,0:T(2,128)}, u32[]{:S(2)}) copy-start(f32[3,2,16384]{2,1,0:T(2,128)} %param.9) | copy-start | bytes 1179652
  1.6 1.0 %copy-start = (bf16[2,2,256,256]{3,2,1,0:T(8,128)(2,1)S(1)}, bf16[2,2,256,256]{3,2,1,0:T(8,128)(2,1)}, u32[]{:S(2)}) copy-start(bf16[2,2,256,256]{3,2,1,0:T(8,128)(2,1)} %constant.4.clone.table_ref) | copy-start | bytes 1572868
  1.6 1.1 %copy-start.1 = (f32[3,8,4096]{2,1,0:T(8,128)S(1)}, f32[3,8,4096]{2,1,0:T(8,128)}, u32[]{:S(2)}) copy-start(f32[3,8,4096]{2,1,0:T(8,128)} %sky_ref.1) | copy-start | bytes 1179652
  1.6 1.2 %copy-start.2 = (f32[4,128,128]{2,1,0:T(8,128)S(1)}, f32[4,128,128]{2,1,0:T(8,128)}, u32[]{:S(2)}) copy-start(f32[4,128,128]{2,1,0:T(8,128)} %constant.5.clone.twiddle_ref) | copy-start | bytes 786436
  1.6 1.2 %copy-start.3 = (s32[6]{0:T(128)S(1)}, s32[6]{0:T(128)}, u32[]{:S(2)}) copy-start(s32[6]{0:T(128)} %cuts_ref.1) | copy-start | bytes 76

commit v2 on v1

--- a/solution.py
+++ b/solution.py
@@ -263,6 +263,7 @@
 
 SIDE = 128
 TILE = (8, 128)
+LEG_GROUPS = ((0, 2), (2, 2), (4, 1))
 MESH = pl.DeviceIdType.MESH
 
 
@@ -360,11 +361,25 @@
         r, f = place(index)
         return {"rows": r, "fields": f}
 
+    half = fields_count // 2
+    my_half, my_spot = my_f // half, my_f % half
+
+    def partner(q, sign):
+        side = (my_half + 1 - q // (rows_count * half)) % 2
+        spot = (my_spot + half + sign * ((q // rows_count + 1) % half)) % half
+        r = (my_r + rows_count + sign * ((q + 1) % rows_count)) % rows_count
+        return r * fields_count + side * half + spot
+
+    def peer_of(q):
+        return partner(q, 1)
+
+    def source_of(q):
+        return partner(q, -1)
+
     def send(q, src, dst, sems):
-        peer = (me + q) % groups
         return pltpu.make_async_remote_copy(
             src_ref=src, dst_ref=dst, send_sem=sems[0], recv_sem=sems[1],
-            device_id=target(peer), device_id_type=MESH,
+            device_id=target(peer_of(q)), device_id_type=MESH,
         )
 
     def send_row(q, src, dst, sems):
@@ -373,17 +388,21 @@
             device_id={"rows": (my_r + q) % rows_count}, device_id_type=MESH,
         )
 
-    def each_peer(body, count=groups):
+    def each_peer(body):
         def step(q, carry):
             body(q)
             return carry
-        lax.fori_loop(1, count, step, 0)
+        lax.fori_loop(0, groups - 1, step, 0)
+
+    def each_row_peer(body):
+        for q in range(1, rows_count):
+            body(q)
 
     barrier = pltpu.get_barrier_semaphore()
 
     def greet(q):
         pl.semaphore_signal(
-            barrier, inc=1, device_id=target((me + q) % groups), device_id_type=MESH
+            barrier, inc=1, device_id=target(peer_of(q)), device_id_type=MESH
         )
 
     each_peer(greet)
@@ -393,22 +412,20 @@
             slab_out[t // 8, field, :, t % 8, :] = sky_ref[field, :, t * SIDE:(t + 1) * SIDE]
     pl.semaphore_wait(barrier, groups - 1)
 
-    def slab_copy(q):
+    def slab_copy(field, q, src_row):
         return send_row(
-            q, slab_out.at[(my_r + q) % rows_count], slab_in.at[my_r],
-            (slab_sem.at[0, q], slab_sem.at[1, q]),
-        )
-
-    def slab_arrival(q):
-        return send_row(
-            q, slab_out.at[(my_r + q) % rows_count],
-            slab_in.at[(my_r + rows_count - q) % rows_count],
-            (slab_sem.at[0, q], slab_sem.at[1, q]),
-        )
-
-    each_peer(lambda q: slab_copy(q).start(), rows_count)
-    own = pltpu.make_async_copy(slab_out.at[my_r], slab_in.at[my_r], self_sem.at[0])
-    own.start()
+            q, slab_out.at[(my_r + q) % rows_count, field], slab_in.at[src_row, field],
+            (slab_sem.at[0, field, q], slab_sem.at[1, field, q]),
+        )
+
+    def own_slab(field):
+        return pltpu.make_async_copy(
+            slab_out.at[my_r, field], slab_in.at[my_r, field], self_sem.at[field]
+        )
+
+    for field in range(3):
+        each_row_peer(lambda q: slab_copy(field, q, my_r).start())
+        own_slab(field).start()
 
     low_index = lax.broadcasted_iota(jnp.int32, (SIDE, SIDE), 0)
     high_index = lax.broadcasted_iota(jnp.int32, (SIDE, SIDE), 1)
@@ -439,75 +456,102 @@
 
     lax.fori_loop(0, local_rows, weigh, 0)
 
-    each_peer(lambda q: slab_arrival(q).wait_recv(), rows_count)
-    own.wait()
-
-    def spec_copy(field, q, src_block):
-        peer = (me + q) % groups
+    def spec_copy(field, row, q, src_block):
         return send(
-            q, spec_out.at[field, peer], spec_in.at[field, :, :, src_block],
-            (spec_sem.at[0, field, q], spec_sem.at[1, field, q]),
-        )
-
-    def own_spec(field):
+            q, spec_out.at[field, row, peer_of(q)], spec_in.at[field, row, :, src_block],
+            (spec_sem.at[0, field, row, q], spec_sem.at[1, field, row, q]),
+        )
+
+    def own_spec(field, row):
         return pltpu.make_async_copy(
-            spec_out.at[field, me], spec_in.at[field, :, :, my_block], self_sem.at[1 + field]
-        )
+            spec_out.at[field, row, me], spec_in.at[field, row, :, my_block],
+            self_sem.at[3 + field * local_rows + row],
+        )
+
+    def spec_start(field, row):
+        each_peer(lambda q: spec_copy(field, row, q, my_block).start())
+        own_spec(field, row).start()
 
     def row_step(field, carry):
+        each_row_peer(
+            lambda q: slab_copy(field, q, (my_r + rows_count - q) % rows_count).wait_recv()
+        )
+        own_slab(field).wait()
         values = [
             (slab_in[y // in_rows, field, y % in_rows], None) for y in range(total_rows)
         ]
         for k, (real, imag) in enumerate(short_transform(values, -1)):
-            spec_out[field, k // local_rows, k % local_rows, 0] = real
-            spec_out[field, k // local_rows, k % local_rows, 1] = (
+            spec_out[field, k % local_rows, k // local_rows, 0] = real
+            spec_out[field, k % local_rows, k // local_rows, 1] = (
                 jnp.zeros_like(real) if imag is None else imag
             )
-        each_peer(lambda q: spec_copy(field, q, my_block).start())
-        own_spec(field).start()
+        spec_start(field, 0)
         return carry
 
     lax.fori_loop(0, 3, row_step, 0)
 
-    def row_wait(field, carry):
-        each_peer(
-            lambda q: spec_copy(field, q, block_of((me + groups - q) % groups)).wait_recv()
-        )
-        own_spec(field).wait()
-        return carry
-
-    lax.fori_loop(0, 3, row_wait, 0)
+    def later_rows(n, carry):
+        spec_start(n % 3, 1 + n // 3)
+        return carry
+
+    lax.fori_loop(0, 3 * (local_rows - 1), later_rows, 0)
+
+    def spec_wait(row):
+        def step(field, carry):
+            each_peer(lambda q: spec_copy(field, row, q, block_of(source_of(q))).wait_recv())
+            own_spec(field, row).wait()
+            return carry
+
+        lax.fori_loop(0, 3, step, 0)
 
     cos_f, sin_f, cos_b, sin_b = 0, 1, 2, 3
 
+    def side_by_side(pieces, axis):
+        return pieces[0] if len(pieces) == 1 else jnp.concatenate(pieces, axis=axis)
+
     def long_forward(pieces):
+        y = matrix_left(table_ref, 0, side_by_side(pieces, 1))
+        c, s = twiddle_ref[cos_f], twiddle_ref[sin_f]
         turned = []
-        for piece in pieces:
-            y = matrix_left(table_ref, 0, piece)
-            yr, yi = y[:SIDE], y[SIDE:]
-            c, s = twiddle_ref[cos_f], twiddle_ref[sin_f]
-            z = jnp.concatenate([yr * c - yi * s, yr * s + yi * c], axis=1)
-            z = matrix_right(table_ref, 1, z)
-            turned.append((z[:, :SIDE], z[:, SIDE:]))
-        return turned
-
-    def long_inverse(pair):
-        u = matrix_right(table_ref, 0, jnp.concatenate([pair[0], pair[1]], axis=1))
-        ur, ui = u[:, :SIDE], u[:, SIDE:]
+        for n in range(len(pieces)):
+            yr, yi = y[:SIDE, n * SIDE:(n + 1) * SIDE], y[SIDE:, n * SIDE:(n + 1) * SIDE]
+            turned.append(jnp.concatenate([yr * c - yi * s, yr * s + yi * c], axis=1))
+        z = matrix_right(table_ref, 1, side_by_side(turned, 0))
+        return [
+            (z[n * SIDE:(n + 1) * SIDE, :SIDE], z[n * SIDE:(n + 1) * SIDE, SIDE:])
+            for n in range(len(pieces))
+        ]
+
+    def long_inverse(pairs):
+        stacks = [jnp.concatenate([pair[0], pair[1]], axis=1) for pair in pairs]
+        u = matrix_right(table_ref, 0, side_by_side(stacks, 0))
         c, s = twiddle_ref[cos_b], twiddle_ref[sin_b]
-        v = jnp.concatenate([ur * c - ui * s, ur * s + ui * c], axis=0)
-        return matrix_left(table_ref, 1, v)
-
-    def legs_copy(row, q, src_index):
-        peer = (me + q) % groups
+        turned = []
+        for n in range(len(pairs)):
+            ur, ui = u[n * SIDE:(n + 1) * SIDE, :SIDE], u[n * SIDE:(n + 1) * SIDE, SIDE:]
+            turned.append(jnp.concatenate([ur * c - ui * s, ur * s + ui * c], axis=0))
+        x = matrix_left(table_ref, 1, side_by_side(turned, 1))
+        return [
+            x[:, n * SIDE:(n + 1) * SIDE].reshape((2, groups) + TILE)
+            for n in range(len(pairs))
+        ]
+
+    leg_self = 3 + 3 * local_rows
+
+    def legs_copy(row, g, q, src_index):
+        first, count = LEG_GROUPS[g]
         return send(
-            q, legs_out.at[row, :, :, block_of(peer)], legs_in.at[row, src_index],
-            (legs_sem.at[0, row, q], legs_sem.at[1, row, q]),
-        )
-
-    def own_legs(row):
+            q, legs_out.at[row, first:first + count, :, block_of(peer_of(q))],
+            legs_in.at[row, src_index, first:first + count],
+            (legs_sem.at[0, row, g, q], legs_sem.at[1, row, g, q]),
+        )
+
+    def own_legs(row, g):
+        first, count = LEG_GROUPS[g]
         return pltpu.make_async_copy(
-            legs_out.at[row, :, :, my_block], legs_in.at[row, me], self_sem.at[4 + row]
+            legs_out.at[row, first:first + count, :, my_block],
+            legs_in.at[row, me, first:first + count],
+            self_sem.at[leg_self + row * len(LEG_GROUPS) + g],
         )
 
     def slopes(row):
@@ -516,6 +560,7 @@
         return along_x, along_y
 
     def leg_step(row, carry):
+        spec_wait(row)
         temp, stokes_q, stokes_u = long_forward(
             [spec_in[field, row].reshape(2 * SIDE, SIDE) for field in range(3)]
         )
@@ -537,20 +582,23 @@
         w = complex_mul((-w_ge * e_bar[0], -w_ge * e_bar[1]), rot)
         h3 = complex_mul(w, raising)
         h1 = complex_mul(w, lowering)
-        for n, leg in enumerate((t_bar, g, p, h3, h1)):
-            legs_out[row, n] = long_inverse(leg).reshape((2, groups) + TILE)
-        each_peer(lambda q: legs_copy(row, q, me).start())
-        own_legs(row).start()
+        legs = (t_bar, g, p, h3, h1)
+        for n, (first, count) in enumerate(LEG_GROUPS):
+            for k, leg_map in enumerate(long_inverse(legs[first:first + count])):
+                legs_out[row, first + k] = leg_map
+            each_peer(lambda q: legs_copy(row, n, q, me).start())
+            own_legs(row, n).start()
         return carry
 
     lax.fori_loop(0, local_rows, leg_step, 0)
 
-    def leg_wait(row, carry):
-        each_peer(lambda q: legs_copy(row, q, (me + groups - q) % groups).wait_recv())
-        own_legs(row).wait()
-        return carry
-
-    lax.fori_loop(0, local_rows, leg_wait, 0)
+    def leg_wait(g):
+        def step(row, carry):
+            each_peer(lambda q: legs_copy(row, g, q, source_of(q)).wait_recv())
+            own_legs(row, g).wait()
+            return carry
+
+        lax.fori_loop(0, local_rows, step, 0)
 
     def map_step(n, carry):
         values = [
@@ -563,7 +611,9 @@
             maps[n, 1, y] = imag
         return carry
 
-    lax.fori_loop(0, 5, map_step, 0)
+    for g, (first, count) in enumerate(LEG_GROUPS):
+        leg_wait(g)
+        lax.fori_loop(first, first + count, map_step, 0)
 
     def product_step(y, carry):
         a, g, p, h3, h1 = [(maps[n, 0, y], maps[n, 1, y]) for n in range(5)]
@@ -576,49 +626,63 @@
 
     values = [(current[0, y], current[1, y]) for y in range(total_rows)]
     for k, (real, imag) in enumerate(short_transform(values, -1)):
-        cur_out[k // local_rows, k % local_rows, 0] = real
-        cur_out[k // local_rows, k % local_rows, 1] = imag
-
-    def cur_copy(q, src_block):
+        cur_out[k % local_rows, k // local_rows, 0] = real
+        cur_out[k % local_rows, k // local_rows, 1] = imag
+    cur_self = leg_self + len(LEG_GROUPS) * local_rows
+    est_self = cur_self + local_rows
+
+    def cur_copy(row, q, src_block):
         return send(
-            q, cur_out.at[(me + q) % groups], cur_in.at[:, :, src_block],
-            (cur_sem.at[0, q], cur_sem.at[1, q]),
-        )
-
-    each_peer(lambda q: cur_copy(q, my_block).start())
-    own_cur = pltpu.make_async_copy(
-        cur_out.at[me], cur_in.at[:, :, my_block], self_sem.at[4 + local_rows]
-    )
-    own_cur.start()
-    each_peer(lambda q: cur_copy(q, block_of((me + groups - q) % groups)).wait_recv())
-    own_cur.wait()
+            q, cur_out.at[row, peer_of(q)], cur_in.at[row, :, src_block],
+            (cur_sem.at[0, row, q], cur_sem.at[1, row, q]),
+        )
+
+    def own_cur(row):
+        return pltpu.make_async_copy(
+            cur_out.at[row, me], cur_in.at[row, :, my_block], self_sem.at[cur_self + row]
+        )
+
+    def cur_start(row, carry):
+        each_peer(lambda q: cur_copy(row, q, my_block).start())
+        own_cur(row).start()
+        return carry
+
+    lax.fori_loop(0, local_rows, cur_start, 0)
+
+    def est_copy(row, q, src_index):
+        return send(
+            q, est_out.at[row, :, block_of(peer_of(q))], est_in.at[row, src_index],
+            (est_sem.at[0, row, q], est_sem.at[1, row, q]),
+        )
+
+    def own_est(row):
+        return pltpu.make_async_copy(
+            est_out.at[row, :, my_block], est_in.at[row, me], self_sem.at[est_self + row]
+        )
 
     def estimate_step(row, carry):
+        each_peer(lambda q: cur_copy(row, q, block_of(source_of(q))).wait_recv())
+        own_cur(row).wait()
         (modes,) = long_forward([cur_in[row].reshape(2 * SIDE, SIDE)])
         along_x, along_y = slopes(row)
         w = weights[5, row]
         estimate = complex_mul((w * modes[0], w * modes[1]), (along_y, along_x))
-        est_out[row] = long_inverse(estimate).reshape((2, groups) + TILE)
+        (est_out[row],) = long_inverse([estimate])
+        each_peer(lambda q: est_copy(row, q, me).start())
+        own_est(row).start()
         return carry
 
     lax.fori_loop(0, local_rows, estimate_step, 0)
 
-    def est_copy(q, src_index):
-        return send(
-            q, est_out.at[:, :, block_of((me + q) % groups)], est_in.at[src_index],
-            (est_sem.at[0, q], est_sem.at[1, q]),
-        )
-
-    each_peer(lambda q: est_copy(q, me).start())
-    own_est = pltpu.make_async_copy(
-        est_out.at[:, :, my_block], est_in.at[me], self_sem.at[5 + local_rows]
-    )
-    own_est.start()
-    each_peer(lambda q: est_copy(q, (me + groups - q) % groups).wait_recv())
-    own_est.wait()
+    def est_wait(row, carry):
+        each_peer(lambda q: est_copy(row, q, source_of(q)).wait_recv())
+        own_est(row).wait()
+        return carry
+
+    lax.fori_loop(0, local_rows, est_wait, 0)
 
     values = [
-        (est_in[k // local_rows, k % local_rows, 0], est_in[k // local_rows, k % local_rows, 1])
+        (est_in[k % local_rows, k // local_rows, 0], est_in[k % local_rows, k // local_rows, 1])
         for k in range(total_rows)
     ]
     for y, (real, imag) in enumerate(short_transform(values, 1)):
@@ -631,35 +695,34 @@
             (fin_sem.at[0, q], fin_sem.at[1, q]),
         )
 
-    each_peer(lambda q: fin_copy(q, my_r).start(), rows_count)
+    each_row_peer(lambda q: fin_copy(q, my_r).start())
     own_fin = pltpu.make_async_copy(
-        fin_out.at[my_r], fin_in.at[my_r], self_sem.at[6 + local_rows]
+        fin_out.at[my_r], fin_in.at[my_r], self_sem.at[est_self + local_rows]
     )
     own_fin.start()
-    each_peer(
-        lambda q: fin_copy(q, (my_r + rows_count - q) % rows_count).wait_recv(), rows_count
-    )
+    each_row_peer(lambda q: fin_copy(q, (my_r + rows_count - q) % rows_count).wait_recv())
     own_fin.wait()
     for part in range(2):
         for t in range(tiles):
             out_ref[part, :, t * SIDE:(t + 1) * SIDE] = fin_in[t // 8, part, :, t % 8, :]
 
-    each_peer(lambda q: slab_copy(q).wait_send(), rows_count)
-
-    def spec_left(field, carry):
-        each_peer(lambda q: spec_copy(field, q, my_block).wait_send())
-        return carry
-
-    lax.fori_loop(0, 3, spec_left, 0)
-
-    def legs_left(row, carry):
-        each_peer(lambda q: legs_copy(row, q, me).wait_send())
-        return carry
-
-    lax.fori_loop(0, local_rows, legs_left, 0)
-    each_peer(lambda q: cur_copy(q, my_block).wait_send())
-    each_peer(lambda q: est_copy(q, me).wait_send())
-    each_peer(lambda q: fin_copy(q, my_r).wait_send(), rows_count)
+    for field in range(3):
+        each_row_peer(lambda q: slab_copy(field, q, my_r).wait_send())
+    each_row_peer(lambda q: fin_copy(q, my_r).wait_send())
+
+    def row_left(row, carry):
+        def spec_left(field, carry):
+            each_peer(lambda q: spec_copy(field, row, q, my_block).wait_send())
+            return carry
+
+        lax.fori_loop(0, 3, spec_left, 0)
+        for g in range(len(LEG_GROUPS)):
+            each_peer(lambda q: legs_copy(row, g, q, me).wait_send())
+        each_peer(lambda q: cur_copy(row, q, my_block).wait_send())
+        each_peer(lambda q: est_copy(row, q, me).wait_send())
+        return carry
+
+    lax.fori_loop(0, local_rows, row_left, 0)
 
 
 def long_tables(total_rows):
@@ -691,7 +754,7 @@
     f32 = jnp.float32
     dma = pltpu.SemaphoreType.DMA
     slab = pltpu.VMEM((rows_count, 3, in_rows) + TILE, f32)
-    chunk = pltpu.VMEM((groups, local_rows, 2) + TILE, f32)
+    chunk = pltpu.VMEM((local_rows, groups, 2) + TILE, f32)
     lines = pltpu.VMEM((local_rows, 2, groups) + TILE, f32)
     final = pltpu.VMEM((rows_count, 2, in_rows) + TILE, f32)
     return pl.pallas_call(
@@ -701,7 +764,7 @@
         out_specs=vmem,
         scratch_shapes=[
             slab, slab,
-            pltpu.VMEM((3, groups, local_rows, 2) + TILE, f32),
+            pltpu.VMEM((3, local_rows, groups, 2) + TILE, f32),
             pltpu.VMEM((3, local_rows, 2, groups) + TILE, f32),
             pltpu.VMEM((6, local_rows, SIDE, SIDE), f32),
             pltpu.VMEM((local_rows, 5, 2, groups) + TILE, f32),
@@ -709,8 +772,10 @@
             pltpu.VMEM((5, 2, total_rows) + TILE, f32),
             pltpu.VMEM((2, total_rows) + TILE, f32),
             chunk, lines, lines, chunk, final, final,
-            dma((2, rows_count)), dma((2, 3, groups)), dma((2, local_rows, groups)),
-            dma((2, groups)), dma((2, groups)), dma((2, rows_count)), dma((7 + local_rows,)),
+            dma((2, 3, rows_count)), dma((2, 3, local_rows, groups - 1)),
+            dma((2, local_rows, len(LEG_GROUPS), groups - 1)),
+            dma((2, local_rows, groups - 1)), dma((2, local_rows, groups - 1)),
+            dma((2, rows_count)), dma((4 + (5 + len(LEG_GROUPS)) * local_rows,)),
         ],
         compiler_params=pltpu.CompilerParams(
             collective_id=0, has_side_effects=True, vmem_limit_bytes=48 * 1024 * 1024
@@ -733,6 +798,7 @@
     def choose(sky_maps, *rest):
         fits = (
             NC == SIDE * SIDE
+            and fields_count % 2 == 0
             and NC // groups == TILE[0] * TILE[1]
             and sky_maps.shape[1] % 8 == 0
             and sky_maps.shape[1] * rows_count in (16, 32, 64)

time: 90.8 us -> 87 us (0.958)
  Pallas kernels: 87.1 us -> 83.3 us
    pallas_call x1, Pallas kernels: 87.1 us -> 83.3 us  [fused_body(): pl.pallas_call(functools.partial(lens_kernel, rows_count, fields_count, l...]
where the time goes in v2:
time: 87 us; the launch traced here: 86.9 us
  Pallas kernels  83.3 us (96%)
  local copies, waits for them, and re-layouts  3.42 us (4%)
    pallas_call x1, Pallas kernels, fused_body(): pl.pallas_call(functools.partial(lens_kernel, rows_count, fields_count, l...  83.3 us
    unnamed x14, local copies, waits for them, and re-layouts  2.86 us

profile of v2, /device:TPU:1, one launch (start us, length us, event | category | flops | bytes accessed | tf_op | source)
XLA Modules:
  0.0 86.9 jit_solution(15134181203900327939)
XLA Ops:
  0.0 0.0 copy-start.5
  0.0 0.0 copy-start.4
  0.0 1.0 %copy.10 = f32[1,2,128,128]{3,2,1,0:T(8,128)S(1)} copy(f32[1,2,128,128]{3,1,2,0:T(2,128)} %bitcast.5) | data formatting | bytes 262144
  1.0 0.0 copy-done.5
  1.0 0.2 concatenate.11
  1.2 0.0 copy-done.4
  1.3 0.3 concatenate.10
  1.6 0.0 copy-start
  1.6 0.0 copy-start.1
  1.6 0.0 copy-start.2
  1.6 0.0 copy-start.3
  1.6 0.1 pad_maximum_fusion.weight_ref
  1.7 0.9 %copy-done = bf16[2,2,256,256]{3,2,1,0:T(8,128)(2,1)S(1)} copy-done((bf16[2,2,256,256]{3,2,1,0:T(8,128)(2,1)S(1)}, bf16[2,2,256,256]{3,2,1,0:T(8,128)(2,1)}, u32[]{:S(2)}) %copy-start) | copy-done | bytes 524312
  2.6 0.1 copy-done.1
  2.8 0.1 copy-done.2
  2.8 0.0 copy-done.3
  2.8 83.3 %lens.1 = f32[2,8,4096]{2,1,0:T(8,128)S(1)} custom-call(s32[6]{0:T(128)S(1)} %copy-done.3, f32[3,8,4096]{2,1,0:T(8,128)S(1)} %copy-done.1, f32[6,2,128,128]{3,2,1,0:T(8,128)S(1)} %pad_maximum_fusion.weight_ref, bf16[2,2,256,256]{3,2,1,0:T(8,128)(2,1)S(1)} %copy-done, f32[4,128,128]{2,1,0:T(8,128)S(1)} %copy-done.2), custom_call_target="tpu_custom_call" | custom-call | tf_op jit(solution)/shard_map/lens/pallas_call | solution.py:760
  86.2 0.7 copy.12
Async XLA Ops:
  0.0 1.0 %copy-start.5 = (f32[2,2,16384]{2,1,0:T(2,128)S(1)}, f32[2,2,16384]{2,1,0:T(2,128)}, u32[]{:S(2)}) copy-start(f32[2,2,16384]{2,1,0:T(2,128)} %param.10) | copy-start | bytes 786436
  0.0 1.2 %copy-start.4 = (f32[3,2,16384]{2,1,0:T(2,128)S(1)}, f32[3,2,16384]{2,1,0:T(2,128)}, u32[]{:S(2)}) copy-start(f32[3,2,16384]{2,1,0:T(2,128)} %param.9) | copy-start | bytes 1179652
  1.6 1.0 %copy-start = (bf16[2,2,256,256]{3,2,1,0:T(8,128)(2,1)S(1)}, bf16[2,2,256,256]{3,2,1,0:T(8,128)(2,1)}, u32[]{:S(2)}) copy-start(bf16[2,2,256,256]{3,2,1,0:T(8,128)(2,1)} %constant.4.clone.table_ref) | copy-start | bytes 1572868
  1.6 1.1 %copy-start.1 = (f32[3,8,4096]{2,1,0:T(8,128)S(1)}, f32[3,8,4096]{2,1,0:T(8,128)}, u32[]{:S(2)}) copy-start(f32[3,8,4096]{2,1,0:T(8,128)} %sky_ref.1) | copy-start | bytes 1179652
  1.6 1.2 %copy-start.2 = (f32[4,128,128]{2,1,0:T(8,128)S(1)}, f32[4,128,128]{2,1,0:T(8,128)}, u32[]{:S(2)}) copy-start(f32[4,128,128]{2,1,0:T(8,128)} %constant.5.clone.twiddle_ref) | copy-start | bytes 786436
  1.6 1.2 %copy-start.3 = (s32[6]{0:T(128)S(1)}, s32[6]{0:T(128)}, u32[]{:S(2)}) copy-start(s32[6]{0:T(128)} %cuts_ref.1) | copy-start | bytes 76

commit v3 on v2

--- a/solution.py
+++ b/solution.py
@@ -350,49 +350,56 @@
     me = my_r * fields_count + my_f
     my_block = my_f * rows_count + my_r
 
-    def place(index):
-        return index // fields_count, index % fields_count
-
-    def block_of(index):
-        r, f = place(index)
-        return f * rows_count + r
-
-    def target(index):
-        r, f = place(index)
-        return {"rows": r, "fields": f}
-
     half = fields_count // 2
     my_half, my_spot = my_f // half, my_f % half
 
+    def wrapped(value, length):
+        return jnp.where(value >= length, value - length, value)
+
+    row_at = [wrapped(my_r + d, rows_count) for d in range(rows_count)]
+    spot_at = [wrapped(my_spot + d, half) for d in range(half)]
+    side_at = [my_half * half, (1 - my_half) * half]
+
     def partner(q, sign):
-        side = (my_half + 1 - q // (rows_count * half)) % 2
-        spot = (my_spot + half + sign * ((q // rows_count + 1) % half)) % half
-        r = (my_r + rows_count + sign * ((q + 1) % rows_count)) % rows_count
-        return r * fields_count + side * half + spot
+        side = 1 - q // (rows_count * half)
+        spot = sign * (q // rows_count + 1) % half
+        return row_at[sign * (q + 1) % rows_count], side_at[side] + spot_at[spot]
 
     def peer_of(q):
-        return partner(q, 1)
+        r, f = partner(q, 1)
+        return r * fields_count + f
 
     def source_of(q):
-        return partner(q, -1)
+        r, f = partner(q, -1)
+        return r * fields_count + f
+
+    def peer_block(q):
+        r, f = partner(q, 1)
+        return f * rows_count + r
+
+    def source_block(q):
+        r, f = partner(q, -1)
+        return f * rows_count + r
+
+    def target(q):
+        r, f = partner(q, 1)
+        return {"rows": r, "fields": f}
 
     def send(q, src, dst, sems):
         return pltpu.make_async_remote_copy(
             src_ref=src, dst_ref=dst, send_sem=sems[0], recv_sem=sems[1],
-            device_id=target(peer_of(q)), device_id_type=MESH,
+            device_id=target(q), device_id_type=MESH,
         )
 
     def send_row(q, src, dst, sems):
         return pltpu.make_async_remote_copy(
             src_ref=src, dst_ref=dst, send_sem=sems[0], recv_sem=sems[1],
-            device_id={"rows": (my_r + q) % rows_count}, device_id_type=MESH,
+            device_id={"rows": row_at[q]}, device_id_type=MESH,
         )
 
     def each_peer(body):
-        def step(q, carry):
+        for q in range(groups - 1):
             body(q)
-            return carry
-        lax.fori_loop(0, groups - 1, step, 0)
 
     def each_row_peer(body):
         for q in range(1, rows_count):
@@ -402,7 +409,7 @@
 
     def greet(q):
         pl.semaphore_signal(
-            barrier, inc=1, device_id=target(peer_of(q)), device_id_type=MESH
+            barrier, inc=1, device_id=target(q), device_id_type=MESH
         )
 
     each_peer(greet)
@@ -414,7 +421,7 @@
 
     def slab_copy(field, q, src_row):
         return send_row(
-            q, slab_out.at[(my_r + q) % rows_count, field], slab_in.at[src_row, field],
+            q, slab_out.at[row_at[q], field], slab_in.at[src_row, field],
             (slab_sem.at[0, field, q], slab_sem.at[1, field, q]),
         )
 
@@ -474,7 +481,7 @@
 
     def row_step(field, carry):
         each_row_peer(
-            lambda q: slab_copy(field, q, (my_r + rows_count - q) % rows_count).wait_recv()
+            lambda q: slab_copy(field, q, row_at[rows_count - q]).wait_recv()
         )
         own_slab(field).wait()
         values = [
@@ -498,7 +505,7 @@
 
     def spec_wait(row):
         def step(field, carry):
-            each_peer(lambda q: spec_copy(field, row, q, block_of(source_of(q))).wait_recv())
+            each_peer(lambda q: spec_copy(field, row, q, source_block(q)).wait_recv())
             own_spec(field, row).wait()
             return carry
 
@@ -541,7 +548,7 @@
     def legs_copy(row, g, q, src_index):
         first, count = LEG_GROUPS[g]
         return send(
-            q, legs_out.at[row, first:first + count, :, block_of(peer_of(q))],
+            q, legs_out.at[row, first:first + count, :, peer_block(q)],
             legs_in.at[row, src_index, first:first + count],
             (legs_sem.at[0, row, g, q], legs_sem.at[1, row, g, q]),
         )
@@ -592,6 +599,15 @@
 
     lax.fori_loop(0, local_rows, leg_step, 0)
 
+    for field in range(3):
+        each_row_peer(lambda q: slab_copy(field, q, my_r).wait_send())
+
+    def spec_left(n, carry):
+        each_peer(lambda q: spec_copy(n % 3, n // 3, q, my_block).wait_send())
+        return carry
+
+    lax.fori_loop(0, 3 * local_rows, spec_left, 0)
+
     def leg_wait(g):
         def step(row, carry):
             each_peer(lambda q: legs_copy(row, g, q, source_of(q)).wait_recv())
@@ -649,9 +665,16 @@
 
     lax.fori_loop(0, local_rows, cur_start, 0)
 
+    def legs_left(row, carry):
+        for g in range(len(LEG_GROUPS)):
+            each_peer(lambda q: legs_copy(row, g, q, me).wait_send())
+        return carry
+
+    lax.fori_loop(0, local_rows, legs_left, 0)
+
     def est_copy(row, q, src_index):
         return send(
-            q, est_out.at[row, :, block_of(peer_of(q))], est_in.at[row, src_index],
+            q, est_out.at[row, :, peer_block(q)], est_in.at[row, src_index],
             (est_sem.at[0, row, q], est_sem.at[1, row, q]),
         )
 
@@ -661,7 +684,7 @@
         )
 
     def estimate_step(row, carry):
-        each_peer(lambda q: cur_copy(row, q, block_of(source_of(q))).wait_recv())
+        each_peer(lambda q: cur_copy(row, q, source_block(q)).wait_recv())
         own_cur(row).wait()
         (modes,) = long_forward([cur_in[row].reshape(2 * SIDE, SIDE)])
         along_x, along_y = slopes(row)
@@ -674,6 +697,12 @@
 
     lax.fori_loop(0, local_rows, estimate_step, 0)
 
+    def cur_left(row, carry):
+        each_peer(lambda q: cur_copy(row, q, my_block).wait_send())
+        return carry
+
+    lax.fori_loop(0, local_rows, cur_left, 0)
+
     def est_wait(row, carry):
         each_peer(lambda q: est_copy(row, q, source_of(q)).wait_recv())
         own_est(row).wait()
@@ -691,7 +720,7 @@
 
     def fin_copy(q, src_row):
         return send_row(
-            q, fin_out.at[(my_r + q) % rows_count], fin_in.at[src_row],
+            q, fin_out.at[row_at[q]], fin_in.at[src_row],
             (fin_sem.at[0, q], fin_sem.at[1, q]),
         )
 
@@ -700,29 +729,19 @@
         fin_out.at[my_r], fin_in.at[my_r], self_sem.at[est_self + local_rows]
     )
     own_fin.start()
-    each_row_peer(lambda q: fin_copy(q, (my_r + rows_count - q) % rows_count).wait_recv())
+
+    def est_left(row, carry):
+        each_peer(lambda q: est_copy(row, q, me).wait_send())
+        return carry
+
+    lax.fori_loop(0, local_rows, est_left, 0)
+    each_row_peer(lambda q: fin_copy(q, row_at[rows_count - q]).wait_recv())
     own_fin.wait()
     for part in range(2):
         for t in range(tiles):
             out_ref[part, :, t * SIDE:(t + 1) * SIDE] = fin_in[t // 8, part, :, t % 8, :]
 
-    for field in range(3):
-        each_row_peer(lambda q: slab_copy(field, q, my_r).wait_send())
     each_row_peer(lambda q: fin_copy(q, my_r).wait_send())
-
-    def row_left(row, carry):
-        def spec_left(field, carry):
-            each_peer(lambda q: spec_copy(field, row, q, my_block).wait_send())
-            return carry
-
-        lax.fori_loop(0, 3, spec_left, 0)
-        for g in range(len(LEG_GROUPS)):
-            each_peer(lambda q: legs_copy(row, g, q, me).wait_send())
-        each_peer(lambda q: cur_copy(row, q, my_block).wait_send())
-        each_peer(lambda q: est_copy(row, q, me).wait_send())
-        return carry
-
-    lax.fori_loop(0, local_rows, row_left, 0)
 
 
 def long_tables(total_rows):

time: 87 us -> 84.9 us (0.976)
  Pallas kernels: 83.3 us -> 81.2 us
    pallas_call x1, Pallas kernels: 83.3 us -> 81.2 us  [fused_body(): pl.pallas_call(functools.partial(lens_kernel, rows_count, fields_count, l...]
where the time goes in v3:
time: 84.9 us; the launch traced here: 84.7 us
  Pallas kernels  81.2 us (96%)
  local copies, waits for them, and re-layouts  3.42 us (4%)
    pallas_call x1, Pallas kernels, fused_body(): pl.pallas_call(functools.partial(lens_kernel, rows_count, fields_count, l...  81.2 us
    unnamed x14, local copies, waits for them, and re-layouts  2.86 us

profile of v3, /device:TPU:1, one launch (start us, length us, event | category | flops | bytes accessed | tf_op | source)
XLA Modules:
  0.0 84.7 jit_solution(2001353124350501065)
XLA Ops:
  0.0 0.0 copy-start.5
  0.0 0.0 copy-start.4
  0.0 1.0 %copy.10 = f32[1,2,128,128]{3,2,1,0:T(8,128)S(1)} copy(f32[1,2,128,128]{3,1,2,0:T(2,128)} %bitcast.5) | data formatting | bytes 262144
  1.0 0.0 copy-done.5
  1.0 0.2 concatenate.11
  1.2 0.0 copy-done.4
  1.3 0.3 concatenate.10
  1.6 0.0 copy-start
  1.6 0.0 copy-start.1
  1.6 0.0 copy-start.2
  1.6 0.0 copy-start.3
  1.6 0.1 pad_maximum_fusion.weight_ref
  1.7 0.9 %copy-done = bf16[2,2,256,256]{3,2,1,0:T(8,128)(2,1)S(1)} copy-done((bf16[2,2,256,256]{3,2,1,0:T(8,128)(2,1)S(1)}, bf16[2,2,256,256]{3,2,1,0:T(8,128)(2,1)}, u32[]{:S(2)}) %copy-start) | copy-done | bytes 524312
  2.6 0.1 copy-done.1
  2.8 0.1 copy-done.2
  2.8 0.0 copy-done.3
  2.8 81.2 %lens.1 = f32[2,8,4096]{2,1,0:T(8,128)S(1)} custom-call(s32[6]{0:T(128)S(1)} %copy-done.3, f32[3,8,4096]{2,1,0:T(8,128)S(1)} %copy-done.1, f32[6,2,128,128]{3,2,1,0:T(8,128)S(1)} %pad_maximum_fusion.weight_ref, bf16[2,2,256,256]{3,2,1,0:T(8,128)(2,1)S(1)} %copy-done, f32[4,128,128]{2,1,0:T(8,128)S(1)} %copy-done.2), custom_call_target="tpu_custom_call" | custom-call | tf_op jit(solution)/shard_map/lens/pallas_call | solution.py:779
  84.0 0.7 copy.12
Async XLA Ops:
  0.0 1.0 %copy-start.5 = (f32[2,2,16384]{2,1,0:T(2,128)S(1)}, f32[2,2,16384]{2,1,0:T(2,128)}, u32[]{:S(2)}) copy-start(f32[2,2,16384]{2,1,0:T(2,128)} %param.10) | copy-start | bytes 786436
  0.0 1.2 %copy-start.4 = (f32[3,2,16384]{2,1,0:T(2,128)S(1)}, f32[3,2,16384]{2,1,0:T(2,128)}, u32[]{:S(2)}) copy-start(f32[3,2,16384]{2,1,0:T(2,128)} %param.9) | copy-start | bytes 1179652
  1.6 1.0 %copy-start = (bf16[2,2,256,256]{3,2,1,0:T(8,128)(2,1)S(1)}, bf16[2,2,256,256]{3,2,1,0:T(8,128)(2,1)}, u32[]{:S(2)}) copy-start(bf16[2,2,256,256]{3,2,1,0:T(8,128)(2,1)} %constant.4.clone.table_ref) | copy-start | bytes 1572868
  1.6 1.1 %copy-start.1 = (f32[3,8,4096]{2,1,0:T(8,128)S(1)}, f32[3,8,4096]{2,1,0:T(8,128)}, u32[]{:S(2)}) copy-start(f32[3,8,4096]{2,1,0:T(8,128)} %sky_ref.1) | copy-start | bytes 1179652
  1.6 1.2 %copy-start.2 = (f32[4,128,128]{2,1,0:T(8,128)S(1)}, f32[4,128,128]{2,1,0:T(8,128)}, u32[]{:S(2)}) copy-start(f32[4,128,128]{2,1,0:T(8,128)} %constant.5.clone.twiddle_ref) | copy-start | bytes 786436
  1.6 1.2 %copy-start.3 = (s32[6]{0:T(128)S(1)}, s32[6]{0:T(128)}, u32[]{:S(2)}) copy-start(s32[6]{0:T(128)} %cuts_ref.1) | copy-start | bytes 76

commit v4 on v3

--- a/solution.py
+++ b/solution.py
@@ -337,10 +337,10 @@
 
 def lens_kernel(
     rows_count, fields_count, local_rows,
-    cuts_ref, sky_ref, weight_ref, table_ref, twiddle_ref, out_ref,
-    slab_out, slab_in, spec_out, spec_in, weights, legs_out, legs_in, maps, current,
+    cuts_ref, sky_hbm, filters_hbm, wiener_hbm, response_hbm, table_ref, twiddle_ref, out_ref,
+    sky_ref, raw, weight_ref, slab_out, slab_in, spec_out, spec_in, weights, legs_out, legs_in, maps, current,
     cur_out, cur_in, est_out, est_in, fin_out, fin_in,
-    slab_sem, spec_sem, legs_sem, cur_sem, est_sem, fin_sem, self_sem,
+    slab_sem, spec_sem, legs_sem, cur_sem, est_sem, fin_sem, self_sem, load_sem,
 ):
     groups = rows_count * fields_count
     total_rows = groups * local_rows
@@ -405,6 +405,18 @@
         for q in range(1, rows_count):
             body(q)
 
+    loads = [
+        pltpu.make_async_copy(src, dst, load_sem.at[n])
+        for n, (src, dst) in enumerate((
+            (sky_hbm, sky_ref),
+            (filters_hbm, raw.at[0:3]),
+            (wiener_hbm, raw.at[3:5]),
+            (response_hbm, raw.at[5]),
+        ))
+    ]
+    for load in loads:
+        load.start()
+
     barrier = pltpu.get_barrier_semaphore()
 
     def greet(q):
@@ -413,6 +425,7 @@
         )
 
     each_peer(greet)
+    loads[0].wait()
     tiles = sky_ref.shape[2] // SIDE
     for field in range(3):
         for t in range(tiles):
@@ -461,7 +474,6 @@
         weights[5, row] = mask(2) * weight_ref[5, row].T
         return carry
 
-    lax.fori_loop(0, local_rows, weigh, 0)
 
     def spec_copy(field, row, q, src_block):
         return send(
@@ -597,6 +609,17 @@
             own_legs(row, n).start()
         return carry
 
+    for load in loads[1:]:
+        load.wait()
+
+    def spread(n, carry):
+        for j in range(8):
+            start = pl.multiple_of((n * 8 + j) * SIDE, SIDE)
+            weight_ref[:, :, n * 8 + j, :] = raw[:, :, pl.ds(start, SIDE)]
+        return carry
+
+    lax.fori_loop(0, SIDE // 8, spread, 0)
+    lax.fori_loop(0, local_rows, weigh, 0)
     lax.fori_loop(0, local_rows, leg_step, 0)
 
     for field in range(3):
@@ -766,9 +789,6 @@
     total_rows = local_rows * groups
     in_rows = total_rows // rows_count
     table, twiddle = long_tables(total_rows)
-    weight = jnp.concatenate([filters, wiener, response[None]]).reshape(
-        6, local_rows, SIDE, SIDE
-    )
     vmem = pl.BlockSpec(memory_space=pltpu.VMEM)
     f32 = jnp.float32
     dma = pltpu.SemaphoreType.DMA
@@ -779,9 +799,14 @@
     return pl.pallas_call(
         functools.partial(lens_kernel, rows_count, fields_count, local_rows),
         out_shape=jax.ShapeDtypeStruct((2,) + sky_maps.shape[1:], f32),
-        in_specs=[pl.BlockSpec(memory_space=pltpu.SMEM)] + [vmem] * 4,
+        in_specs=[pl.BlockSpec(memory_space=pltpu.SMEM)]
+        + [pl.BlockSpec(memory_space=pl.ANY)] * 4
+        + [vmem] * 2,
         out_specs=vmem,
         scratch_shapes=[
+            pltpu.VMEM(sky_maps.shape, f32),
+            pltpu.VMEM((6, local_rows, NC), f32),
+            pltpu.VMEM((6, local_rows, SIDE, SIDE), f32),
             slab, slab,
             pltpu.VMEM((3, local_rows, groups, 2) + TILE, f32),
             pltpu.VMEM((3, local_rows, 2, groups) + TILE, f32),
@@ -795,12 +820,13 @@
             dma((2, local_rows, len(LEG_GROUPS), groups - 1)),
             dma((2, local_rows, groups - 1)), dma((2, local_rows, groups - 1)),
             dma((2, rows_count)), dma((4 + (5 + len(LEG_GROUPS)) * local_rows,)),
+            dma((4,)),
         ],
         compiler_params=pltpu.CompilerParams(
-            collective_id=0, has_side_effects=True, vmem_limit_bytes=48 * 1024 * 1024
+            collective_id=0, has_side_effects=True, vmem_limit_bytes=60 * 1024 * 1024
         ),
         name="lens",
-    )(band_cuts, sky_maps, weight, jnp.asarray(table), jnp.asarray(twiddle))
+    )(band_cuts, sky_maps, filters, wiener, response, jnp.asarray(table), jnp.asarray(twiddle))
 
 
 def solution(mesh):

time: 84.9 us -> 84.4 us (level)
  local copies, waits for them, and re-layouts: 3.42 us -> 1.67 us
  Pallas kernels: 81.2 us -> 82.5 us
    pallas_call x1, Pallas kernels: 81.2 us -> 82.5 us  [fused_body(): pl.pallas_call(functools.partial(lens_kernel, rows_count, fields_count, l...]
    unnamed x14 -> x1, local copies, waits for them, and re-layouts: 2.86 us -> 1.67 us
where the time goes in v4:
time: 84.4 us; the launch traced here: 84.2 us
  Pallas kernels  82.5 us (98%)
  local copies, waits for them, and re-layouts  1.67 us (2%)
    pallas_call x1, Pallas kernels, fused_body(): pl.pallas_call(functools.partial(lens_kernel, rows_count, fields_count, l...  82.5 us

profile of v4, /device:TPU:1, one launch (start us, length us, event | category | flops | bytes accessed | tf_op | source)
XLA Modules:
  0.0 84.2 jit_solution(115117369393550211)
XLA Ops:
  0.0 82.5 %lens.1 = f32[2,8,4096]{2,1,0:T(8,128)} custom-call(s32[6]{0:T(128)} %cuts_ref.1, f32[3,8,4096]{2,1,0:T(8,128)} %sky_hbm.1, f32[3,2,16384]{2,1,0:T(2,128)} %filters_hbm.1, f32[2,2,16384]{2,1,0:T(2,128)} %wiener_hbm.1, f32[2,16384]{1,0:T(2,128)} %response_hbm.1, bf16[2,2,256,256]{3,2,1,0:T(8,128)(2,1)} %constant.4.clone.table_ref, ...), custom_call_target="tpu_custom_call" | custom-call | tf_op jit(solution)/shard_map/lens/pallas_call | solution.py:799
  82.5 1.7 %copy.9 = f32[2,8,4096]{2,1,0:T(8,128)} copy(f32[2,8,4096]{2,1,0:T(8,128)} %lens.1) | data formatting | bytes 524288
